TPU v7x, 32 devices: a whole 2x2x4 slice. The times are simulated.
32 devices in a mesh: dp: 2 (over x), col: 4 (over z), row: 4 (over y, core).
Axes of the slice: x: 2, y: 2, z: 4, core: 2. Of those that a mesh axis runs over, the one named last changes fastest.
Arguments:
- hidden: bfloat16 [128, 3584], P('dp', 'row'), parts along dimension 0
- norm_gain: float32 [3584], P('row')
- w_head: bfloat16 [3584, 152064], P('row', 'col')
Outputs:
- output 1: float32 [128, 152064], P('dp', ('col', 'row')), parts along dimension 0
- output 2: float32 [128], P('dp'), parts along dimension 0
There are 2 independent parts. A program takes and returns all parts, laid end to end along the dimension named above; an argument that names none is the same for every part.
All inputs are finite; a program needn't handle non-finite values.
Results may differ from a plain program's by a relative error of at most 0.001.
Values sent between devices are 32-bit elements.
A program may use at most 1 GiB of HBM per device.

v0:
```python
import jax
import jax.numpy as jnp
from jax import lax
from jax.sharding import PartitionSpec as P

EPS = 1e-5


def solution(mesh):
    row_count = mesh.shape["row"]

    def local_head(hidden, norm_gain, w_head):
        wide_hidden = hidden.astype(jnp.float32)
        local_sq = jnp.sum(wide_hidden * wide_hidden, axis=-1, keepdims=True)
        total_sq = lax.psum(local_sq, "row")
        mean_sq = total_sq / (hidden.shape[1] * row_count)
        normed = (wide_hidden * lax.rsqrt(mean_sq + EPS) * norm_gain).astype(jnp.bfloat16)
        share_logits = jnp.dot(normed, w_head, preferred_element_type=jnp.float32)
        logits = lax.psum_scatter(share_logits, "row", scatter_dimension=1, tiled=True)
        local_max = jnp.max(logits, axis=-1, keepdims=True)
        global_max = lax.pmax(local_max, ("col", "row"))
        local_mass = jnp.sum(jnp.exp(logits - global_max), axis=-1, keepdims=True)
        total_mass = lax.psum(local_mass, ("col", "row"))
        log_norm = global_max + jnp.log(total_mass)
        return logits - log_norm, log_norm[:, 0]

    return jax.shard_map(
        local_head,
        mesh=mesh,
        in_specs=(P("dp", "row"), P("row"), P("row", "col")),
        out_specs=(P("dp", ("col", "row")), P("dp")),
        check_vma=False,
    )
```

profile of v0, /device:TPU:0, one launch (start us, length us, event | category | flops | bytes accessed | tf_op | source)
XLA Modules:
  0.0 269.9 jit_solution(14025207750227466044)
XLA Ops:
  7.2 0.0 reduce-scatter.4.cloned.1.call-start
  7.2 1.0 fusion
  8.2 8.4 %psum.14 = f32[64,1]{0,1:T(1,128)S(1)} all-reduce(f32[64,1]{0,1:T(1,128)S(1)} %bitcast.15), channel_id=1, replica_groups=mesh['dp'=2,'col'=4,'row'=4] {'row'}, use_global_device_ids=true, to_apply=%region_1.0 | all-reduce | flops 64 | bytes 512 | tf_op jit(solution)/shard_map/psum | solution.py:15
  16.7 34.9 %convolution_bitcast_fusion = f32[38016,64]{1,0:T(8,128)} fusion(bf16[896,38016]{1,0:T(8,128)(2,1)} %param.5, bf16[64,896]{1,0:T(8,128)(2,1)} %param.3, f32[896]{0:T(1024)} %param.4, f32[64]{0:T(128)S(1)} %rsqrt_bitcast_fusion), kind=kOutput, calls=%fused_computation | convolution fusion | flops 4360208384 | bytes 77975296
  51.6 0.0 reduce-scatter.4.cloned.1.call-update
  51.6 140.9 %reduce-scatter.4.cloned.1.call-done = f32[9504,64]{1,0:T(8,128)} async-done(((f32[38016,64]{1,0:T(8,128)}), f32[9504,64]{1,0:T(8,128)}) %reduce-scatter.4.cloned.1.call-update) | async-done | bytes 2433040
  192.5 3.1 %bitcast_reduce_fusion = f32[64]{0:T(128)S(1)} fusion(f32[9504,64]{1,0:T(8,128)} %reduce-scatter.4.cloned.1.call-done), kind=kLoop, calls=%fused_computation.12 | loop fusion | flops 608192 | bytes 2433280 | tf_op jit(solution)/shard_map/reduce_max | solution.py:20
  195.5 32.0 %pmax.7 = f32[64,1]{0,1:T(1,128)S(1)} all-reduce(f32[64,1]{0,1:T(1,128)S(1)} %bitcast.16), channel_id=1, replica_groups=mesh['dp'=2,'col'=4,'row'=4] {'col','row'}, use_global_device_ids=true, to_apply=%region_4.0 | all-reduce | flops 64 | bytes 512 | tf_op jit(solution)/shard_map/pmax | solution.py:21
  227.5 3.8 %copy.6 = f32[64,9504]{1,0:T(8,128)S(1)} copy(f32[64,9504]{0,1:T(8,128)} %bitcast.13) | data formatting | bytes 4866048
  231.3 0.6 exponential_reduce_fusion
  231.9 29.5 %psum.15 = f32[64,1]{0,1:T(1,128)S(1)} all-reduce(f32[64,1]{0,1:T(1,128)S(1)} %bitcast.17), channel_id=1, replica_groups=mesh['dp'=2,'col'=4,'row'=4] {'col','row'}, use_global_device_ids=true, to_apply=%region_6.0 | all-reduce | flops 64 | bytes 512 | tf_op jit(solution)/shard_map/psum | solution.py:23
  261.4 0.0 copy-start
  261.4 1.7 broadcast_subtract_fusion
  263.1 0.0 copy-done
  (2 shorter events, 0.0 us)
Async XLA Ops:
  7.2 185.3 %reduce-scatter.4.cloned.1.call-start = ((), (), s32[]{:S(2)}) async-start(), calls=%async_computation.1 | async-start | bytes 24330240
  261.4 1.7 copy-start
Sparse Core Ops, SparseCore 0:
  51.7 140.7 reduce-scatter.3
where the time goes:
time: 270 us
  waiting for transfers between devices  141 us (52%)
  blocking collectives  69.9 us (26%)
  matrix products  34.9 us (13%)
  between operations  14 us (5%)
  other arithmetic  6.32 us (2%)
  local copies, waits for them, and re-layouts  3.82 us (1%)
    unnamed x2, waiting for transfers between devices  141 us
    unnamed x1, matrix products  34.9 us
    pmax x1, blocking collectives, local_head(): global_max = lax.pmax(local_max, ('col', 'row'))  32 us
    psum x1, blocking collectives, local_head(): total_mass = lax.psum(local_mass, ('col', 'row'))  29.5 us
    psum x1, blocking collectives, local_head(): total_sq = lax.psum(local_sq, 'row')  8.44 us
  transfers between devices with their start and end apart: 1, of which 1 were waited for; matrix products, arithmetic and copies ran while one was open for 0% of the time, Pallas kernels for 0%

commit v1 on v0

v1 whole, which is shorter than its diff:
```python
import jax
import jax.numpy as jnp
from jax import lax
from jax.experimental import pallas as pl
from jax.experimental.pallas import tpu as pltpu
from jax.sharding import PartitionSpec as P

EPS = 1e-5
MESH = pl.DeviceIdType.MESH
LANES = 128
TILES = 3
CHUNK = TILES * LANES
SLOTS = 12


def head_kernel(
    count, width, hidden_size,
    h_ref, g_ref, w_ref, z_ref, lse_ref,
    wa, wb, x_ref, qbuf, rbuf, pbuf, lbuf, rin, lin, yin, nst, fst, m_ref, s_ref, carry,
    wa_sem, wb_sem, nsend, nrecv, qsend, psend, ysend, rrecv, lrecv, yrecv, fsend, frecv,
):
    rows = h_ref.shape[0]
    feats = h_ref.shape[1]
    stride = (width // LANES) * LANES
    rest = width - stride
    col = lax.axis_index("col")
    row = lax.axis_index("row")
    core = lax.rem(row, 2)
    mate = row + 1 - 2 * core
    across = lax.rem(row + 2, 4)
    far = 3 - row
    shift = row * rest

    def fetch(stream, t):
        if stream == 0:
            first, second, buf, sem = far, mate, wa, wa_sem
        else:
            first, second, buf, sem = across, row, wb, wb_sem
        part = first + (second - first) * (t // count)
        start = pl.multiple_of(stride * part + CHUNK * lax.rem(t, count), LANES)
        slot = lax.rem(t, SLOTS)
        return pltpu.make_async_copy(w_ref.at[:, pl.ds(start, CHUNK)], buf.at[slot], sem.at[slot])

    for t in range(SLOTS):
        fetch(0, t).start()
        fetch(1, t).start()

    barrier = pltpu.get_barrier_semaphore()
    for dc in range(4):
        for dr in range(4):
            if dc or dr:
                pl.semaphore_signal(
                    barrier, inc=1, device_id_type=MESH,
                    device_id={"col": lax.rem(col + dc, 4), "row": lax.rem(row + dr, 4)},
                )

    lane = lax.broadcasted_iota(jnp.int32, (rows, LANES), 1)
    sq = jnp.zeros((rows, LANES), jnp.float32)
    for j in range(feats // LANES):
        part = h_ref[:, j * LANES:(j + 1) * LANES].astype(jnp.float32)
        sq = sq + part * part
    sq = jnp.transpose(jnp.concatenate([sq, sq], axis=0))
    nst[row] = jnp.sum(sq, axis=0, keepdims=True)
    pl.semaphore_wait(barrier, 15)

    def norm_copy(k):
        return pltpu.make_async_remote_copy(
            src_ref=nst.at[row], dst_ref=nst.at[row], send_sem=nsend.at[k], recv_sem=nrecv.at[row],
            device_id={"row": lax.rem(row + k, 4)}, device_id_type=MESH,
        )

    for k in range(1, 4):
        norm_copy(k).start()
    for k in range(1, 4):
        peer = lax.rem(row + k, 4)
        pltpu.make_async_remote_copy(
            src_ref=nst.at[peer], dst_ref=nst.at[peer], send_sem=nsend.at[k], recv_sem=nrecv.at[peer],
            device_id={"row": peer}, device_id_type=MESH,
        ).wait_recv()
    total = nst[0] + nst[1] + nst[2] + nst[3]
    scale = lax.rsqrt(total / hidden_size + EPS)
    scale = jnp.transpose(jnp.broadcast_to(scale, (LANES, LANES)))[:rows]
    for j in range(feats // LANES):
        cols = slice(j * LANES, (j + 1) * LANES)
        x_ref[:, cols] = (h_ref[:, cols].astype(jnp.float32) * scale * g_ref[:, cols]).astype(jnp.bfloat16)

    def product(stream, t):
        buf, sem = ((wa, wa_sem), (wb, wb_sem))[stream]
        fetch(stream, t).wait()
        slot = lax.rem(t, SLOTS)
        return jnp.dot(x_ref[...], buf[slot], preferred_element_type=jnp.float32)

    def refill(stream, t):
        @pl.when(t + SLOTS < 2 * count)
        def _():
            fetch(stream, t + SLOTS).start()

    def mate_copy(src, dst, send, recv, i):
        return pltpu.make_async_remote_copy(
            src_ref=src.at[i], dst_ref=dst.at[i], send_sem=send, recv_sem=recv.at[i],
            device_id={"row": mate}, device_id_type=MESH,
        )

    def across_copy(i):
        return pltpu.make_async_remote_copy(
            src_ref=rbuf.at[i], dst_ref=yin.at[i], send_sem=ysend, recv_sem=yrecv.at[i],
            device_id={"row": across}, device_id_type=MESH,
        )

    def far_step(i):
        qbuf[i] = product(0, i)
        mate_copy(qbuf, rin, qsend, rrecv, i).start()
        refill(0, i)

    def across_step(i):
        term = product(1, i)
        refill(1, i)
        mate_copy(qbuf, rin, qsend, rrecv, i).wait_recv()
        rbuf[i] = term + rin[i]
        across_copy(i).start()

    far_step(0)

    @pl.loop(0, count - 1)
    def _(i):
        far_step(i + 1)
        across_step(i)

    across_step(count - 1)

    @pl.loop(0, count)
    def _(i):
        pbuf[i] = product(0, count + i)
        mate_copy(pbuf, lin, psend, lrecv, i).start()
        refill(0, count + i)
        lbuf[i] = product(1, count + i)
        refill(1, count + i)

    turn = lax.rem(LANES - shift, LANES)
    keep = lane < LANES - shift

    def turned(i):
        mate_copy(pbuf, lin, psend, lrecv, i).wait_recv()
        across_copy(i).wait_recv()
        full = lbuf[i] + lin[i] + yin[i]
        return [pltpu.roll(full[:, k * LANES:(k + 1) * LANES], turn, 1) for k in range(TILES)]

    def arrive(i, first):
        rolled = turned(i)
        tiles = [jnp.where(keep, rolled[k], rolled[k + 1]) for k in range(TILES - 1)]
        at = 0
        if not first:
            tiles = [jnp.where(keep, carry[...], rolled[0])] + tiles
            at = pl.multiple_of(i * CHUNK - LANES, LANES)
        carry[...] = rolled[-1]
        z_ref[:, pl.ds(at, LANES * len(tiles))] = jnp.concatenate(tiles, axis=1)
        top = tiles[0]
        for tile in tiles[1:]:
            top = jnp.maximum(top, tile)
        if not first:
            top = jnp.maximum(top, m_ref[...])
        mass = jnp.exp(tiles[0] - top)
        for tile in tiles[1:]:
            mass = mass + jnp.exp(tile - top)
        if not first:
            mass = mass + s_ref[...] * jnp.exp(m_ref[...] - top)
        m_ref[...] = top
        s_ref[...] = mass

    arrive(0, True)

    @pl.loop(1, count)
    def _(i):
        arrive(i, False)

    last = carry[...]
    z_ref[:, stride:] = last[:, :rest]
    last = jnp.where(lane < rest, last, -jnp.inf)
    top = jnp.maximum(m_ref[...], last)
    mass = s_ref[...] * jnp.exp(m_ref[...] - top) + jnp.exp(last - top)
    top = jnp.transpose(jnp.concatenate([top, top], axis=0))
    mass = jnp.transpose(jnp.concatenate([mass, mass], axis=0))
    peak = jnp.max(top, axis=0, keepdims=True)
    mass = jnp.sum(mass * jnp.exp(top - peak), axis=0, keepdims=True)
    me = col * 4 + row
    fst[me] = jnp.where(lane[:1] < rows, peak, mass)

    def stat_copy(dc, dr):
        k = dc * 4 + dr
        return pltpu.make_async_remote_copy(
            src_ref=fst.at[me], dst_ref=fst.at[me], send_sem=fsend.at[k], recv_sem=frecv.at[me],
            device_id={"col": lax.rem(col + dc, 4), "row": lax.rem(row + dr, 4)}, device_id_type=MESH,
        )

    peers = [(dc, dr) for dc in (3, 2, 1, 0) for dr in (2, 3, 1, 0) if dc or dr]
    for dc, dr in peers:
        stat_copy(dc, dr).start()
    for dc, dr in peers:
        pc, pr = lax.rem(col + dc, 4), lax.rem(row + dr, 4)
        peer = pc * 4 + pr
        pltpu.make_async_remote_copy(
            src_ref=fst.at[peer], dst_ref=fst.at[peer], send_sem=fsend.at[dc * 4 + dr], recv_sem=frecv.at[peer],
            device_id={"col": pc, "row": pr}, device_id_type=MESH,
        ).wait_recv()
    stats = fst[...]
    swapped = pltpu.roll(stats, LANES // 2, 2)
    peak = jnp.max(stats, axis=0)
    mass = jnp.sum(swapped * jnp.exp(stats - peak), axis=0)
    lse_ref[...] = peak + jnp.log(mass)

    for k in range(1, 4):
        norm_copy(k).wait_send()
    for src, dst, send, recv in ((qbuf, rin, qsend, rrecv), (pbuf, lin, psend, lrecv)):
        pltpu.make_async_remote_copy(
            src_ref=src, dst_ref=dst, send_sem=send, recv_sem=recv.at[0],
            device_id={"row": mate}, device_id_type=MESH,
        ).wait_send()
    pltpu.make_async_remote_copy(
        src_ref=rbuf, dst_ref=yin, send_sem=ysend, recv_sem=yrecv.at[0],
        device_id={"row": across}, device_id_type=MESH,
    ).wait_send()
    for dc, dr in peers:
        stat_copy(dc, dr).wait_send()


def solution(mesh):
    def local_head(hidden, norm_gain, w_head):
        rows, feats = hidden.shape
        width = w_head.shape[1] // 4
        count = (width // LANES + 1) // TILES
        block = (count, rows, CHUNK)
        dma = pltpu.SemaphoreType.DMA

        def body(*refs):
            head_kernel(count, width, feats * 4, *refs)

        z, lse = pl.pallas_call(
            body,
            out_shape=(
                jax.ShapeDtypeStruct((rows, width), jnp.float32),
                jax.ShapeDtypeStruct((1, LANES), jnp.float32),
            ),
            in_specs=[
                pl.BlockSpec(memory_space=pltpu.VMEM),
                pl.BlockSpec(memory_space=pltpu.VMEM),
                pl.BlockSpec(memory_space=pl.ANY),
            ],
            out_specs=(pl.BlockSpec(memory_space=pltpu.VMEM), pl.BlockSpec(memory_space=pltpu.VMEM)),
            scratch_shapes=[
                pltpu.VMEM((SLOTS, feats, CHUNK), jnp.bfloat16),
                pltpu.VMEM((SLOTS, feats, CHUNK), jnp.bfloat16),
                pltpu.VMEM((rows, feats), jnp.bfloat16),
                *[pltpu.VMEM(block, jnp.float32) for _ in range(7)],
                pltpu.VMEM((4, 1, LANES), jnp.float32),
                pltpu.VMEM((16, 1, LANES), jnp.float32),
                *[pltpu.VMEM((rows, LANES), jnp.float32) for _ in range(3)],
                dma((SLOTS,)), dma((SLOTS,)), dma((4,)), dma((4,)),
                dma, dma, dma, dma((count,)), dma((count,)), dma((count,)), dma((16,)), dma((16,)),
            ],
            compiler_params=pltpu.CompilerParams(
                collective_id=0, has_side_effects=True, vmem_limit_bytes=48 * 1024 * 1024
            ),
            name="head",
        )(hidden, norm_gain.reshape(1, feats), w_head)
        log_norm = lse[0, :rows]
        return z - log_norm[:, None], log_norm

    return jax.shard_map(
        local_head,
        mesh=mesh,
        in_specs=(P("dp", "row"), P("row"), P("row", "col")),
        out_specs=(P("dp", ("col", "row")), P("dp")),
        check_vma=False,
    )
```

time: 270 us -> 73.2 us (0.27)
  waiting for transfers between devices: 141 us -> 0 us
  blocking collectives: 69.9 us -> 0 us
  Pallas kernels: 0 us -> 69.1 us
  matrix products: 34.9 us -> 0 us
  between operations: 14 us -> 0.66 us
  other arithmetic: 6.32 us -> 1.67 us
    unnamed x2 -> x0, waiting for transfers between devices: 141 us -> none
    pallas_call x0 -> x1, Pallas kernels: none -> 69.1 us  [local_head(): pl.pallas_call(body, out_shape=(jax.ShapeDtypeStruct((rows, width), jnp.f...]
    psum x2 -> x0, blocking collectives: 37.9 us -> none  [the longest x1 29.5 us: local_head(): total_mass = lax.psum(local_mass, ('col', 'row'))]
    unnamed x1 -> x0, matrix products: 34.9 us -> none
    pmax x1 -> x0, blocking collectives: 32 us -> none  [local_head(): global_max = lax.pmax(local_max, ('col', 'row'))]
    reduce_max x1 -> x0, other arithmetic: 3.06 us -> none  [local_head(): local_max = jnp.max(logits, axis=-1, keepdims=True)]
    unnamed x3 -> x4, local copies, waits for them, and re-layouts: 3.82 us -> 0.9 us
  transfers between devices with their start and end apart: 1 -> 0, of which waited for: 1 -> 0; matrix products, arithmetic and copies ran while one was open for 0% -> 0% of each run, Pallas kernels for 0% -> 0%
where the time goes in v1:
time: 73.2 us; the launch traced here: 73.1 us
  Pallas kernels  69.1 us (94%)
  other arithmetic  1.67 us (2%)
  local copies, waits for them, and re-layouts  1.6 us (2%)
    pallas_call x1, Pallas kernels, local_head(): pl.pallas_call(body, out_shape=(jax.ShapeDtypeStruct((rows, width), jnp.f...  69.1 us
    sub x1, other arithmetic, local_head(): return (z - log_norm[:, None], log_norm)  1.67 us

profile of v1, /device:TPU:0, one launch (start us, length us, event | category | flops | bytes accessed | tf_op | source)
XLA Modules:
  0.0 73.1 jit_solution(18214727810473230122)
XLA Ops:
  0.6 0.7 reshape.8.refs_1_
  1.3 0.0 copy-start
  1.3 0.9 %copy-done = bf16[64,896]{1,0:T(8,128)(2,1)S(1)} copy-done((bf16[64,896]{1,0:T(8,128)(2,1)S(1)}, bf16[64,896]{1,0:T(8,128)(2,1)}, u32[]{:S(2)}) %copy-start) | copy-done | bytes 114712
  2.2 69.1 %head.1 = (f32[64,9504]{1,0:T(8,128)S(1)}, f32[1,128]{1,0:T(1,128)S(1)}) custom-call(bf16[64,896]{1,0:T(8,128)(2,1)S(1)} %copy-done, f32[1,896]{1,0:T(1,128)S(1)} %reshape.8.refs_1_, bf16[896,38016]{1,0:T(8,128)(2,1)} %refs_2_.1), custom_call_target="tpu_custom_call" | custom-call | tf_op jit(solution)/shard_map/head/pallas_call | solution.py:237
  71.4 0.0 copy-start.1
  71.4 1.7 %broadcast_subtract_fusion = f32[64,9504]{1,0:T(8,128)} fusion(f32[64,9504]{1,0:T(8,128)S(1)} %get-tuple-element.4, f32[64]{0:T(128)S(1)} %slice_bitcast_fusion), kind=kLoop, calls=%fused_computation | loop fusion | flops 608256 | bytes 4866304 | tf_op jit(solution)/shard_map/sub | solution.py:266
  73.1 0.0 copy-done.1
  (1 shorter events, 0.0 us)
Async XLA Ops:
  1.3 0.9 %copy-start = (bf16[64,896]{1,0:T(8,128)(2,1)S(1)}, bf16[64,896]{1,0:T(8,128)(2,1)}, u32[]{:S(2)}) copy-start(bf16[64,896]{1,0:T(8,128)(2,1)} %refs_0_.1) | copy-start | bytes 344068
  71.4 1.7 %copy-start.1 = (f32[64]{0:T(128)}, f32[64]{0:T(128)S(1)}, u32[]{:S(2)}) copy-start(f32[64]{0:T(128)S(1)} %slice_bitcast_fusion) | copy-start | bytes 772

commit v2 on v1

--- a/solution.py
+++ b/solution.py
@@ -15,12 +15,11 @@
 
 def head_kernel(
     count, width, hidden_size,
-    h_ref, g_ref, w_ref, z_ref, lse_ref,
-    wa, wb, x_ref, qbuf, rbuf, pbuf, lbuf, rin, lin, yin, nst, fst, m_ref, s_ref, carry,
-    wa_sem, wb_sem, nsend, nrecv, qsend, psend, ysend, rrecv, lrecv, yrecv, fsend, frecv,
+    h_hbm, g_hbm, w_ref, z_ref, lse_ref,
+    h_ref, g_ref, wa, wb, x_ref, qbuf, rbuf, pbuf, lbuf, rin, lin, yin, nst, fst, m_ref, s_ref, carry,
+    h_sem, g_sem, hops, wa_sem, wb_sem, nsend, nrecv, qsend, psend, ysend, rrecv, lrecv, yrecv, fsend, frecv,
 ):
-    rows = h_ref.shape[0]
-    feats = h_ref.shape[1]
+    rows, feats = h_ref.shape
     stride = (width // LANES) * LANES
     rest = width - stride
     col = lax.axis_index("col")
@@ -41,18 +40,27 @@
         slot = lax.rem(t, SLOTS)
         return pltpu.make_async_copy(w_ref.at[:, pl.ds(start, CHUNK)], buf.at[slot], sem.at[slot])
 
+    barrier = pltpu.get_barrier_semaphore()
+
+    def tell_columns(sem):
+        for step, there in ((-1, col > 0), (1, col < 3)):
+            @pl.when(there)
+            def _():
+                pl.semaphore_signal(sem, inc=1, device_id_type=MESH, device_id={"col": col + step})
+
+    for k in (2, 3, 1):
+        pl.semaphore_signal(barrier, inc=1, device_id_type=MESH, device_id={"row": lax.rem(row + k, 4)})
+    tell_columns(barrier)
+    beside = (col + 2) // 3 + (5 - col) // 3
+
+    h_copy = pltpu.make_async_copy(h_hbm, h_ref, h_sem)
+    g_copy = pltpu.make_async_copy(g_hbm, g_ref, g_sem)
+    h_copy.start()
+    g_copy.start()
     for t in range(SLOTS):
         fetch(0, t).start()
         fetch(1, t).start()
-
-    barrier = pltpu.get_barrier_semaphore()
-    for dc in range(4):
-        for dr in range(4):
-            if dc or dr:
-                pl.semaphore_signal(
-                    barrier, inc=1, device_id_type=MESH,
-                    device_id={"col": lax.rem(col + dc, 4), "row": lax.rem(row + dr, 4)},
-                )
+    h_copy.wait()
 
     lane = lax.broadcasted_iota(jnp.int32, (rows, LANES), 1)
     sq = jnp.zeros((rows, LANES), jnp.float32)
@@ -61,7 +69,7 @@
         sq = sq + part * part
     sq = jnp.transpose(jnp.concatenate([sq, sq], axis=0))
     nst[row] = jnp.sum(sq, axis=0, keepdims=True)
-    pl.semaphore_wait(barrier, 15)
+    pl.semaphore_wait(barrier, 3 + beside)
 
     def norm_copy(k):
         return pltpu.make_async_remote_copy(
@@ -77,12 +85,14 @@
             src_ref=nst.at[peer], dst_ref=nst.at[peer], send_sem=nsend.at[k], recv_sem=nrecv.at[peer],
             device_id={"row": peer}, device_id_type=MESH,
         ).wait_recv()
+    tell_columns(hops.at[0])
+    g_copy.wait()
     total = nst[0] + nst[1] + nst[2] + nst[3]
     scale = lax.rsqrt(total / hidden_size + EPS)
     scale = jnp.transpose(jnp.broadcast_to(scale, (LANES, LANES)))[:rows]
     for j in range(feats // LANES):
         cols = slice(j * LANES, (j + 1) * LANES)
-        x_ref[:, cols] = (h_ref[:, cols].astype(jnp.float32) * scale * g_ref[:, cols]).astype(jnp.bfloat16)
+        x_ref[:, cols] = (h_ref[:, cols].astype(jnp.float32) * scale * g_ref[cols].reshape(1, LANES)).astype(jnp.bfloat16)
 
     def product(stream, t):
         buf, sem = ((wa, wa_sem), (wb, wb_sem))[stream]
@@ -127,6 +137,8 @@
         across_step(i)
 
     across_step(count - 1)
+    pl.semaphore_wait(hops.at[0], beside)
+    tell_columns(hops.at[1])
 
     @pl.loop(0, count)
     def _(i):
@@ -135,6 +147,9 @@
         refill(0, count + i)
         lbuf[i] = product(1, count + i)
         refill(1, count + i)
+
+    pl.semaphore_wait(hops.at[1], beside)
+    tell_columns(hops.at[2])
 
     turn = lax.rem(LANES - shift, LANES)
     keep = lane < LANES - shift
@@ -168,6 +183,7 @@
         s_ref[...] = mass
 
     arrive(0, True)
+    pl.semaphore_wait(hops.at[2], beside)
 
     @pl.loop(1, count)
     def _(i):
@@ -241,12 +257,14 @@
                 jax.ShapeDtypeStruct((1, LANES), jnp.float32),
             ),
             in_specs=[
-                pl.BlockSpec(memory_space=pltpu.VMEM),
-                pl.BlockSpec(memory_space=pltpu.VMEM),
-                pl.BlockSpec(memory_space=pl.ANY),
+                pl.BlockSpec(memory_space=pltpu.HBM),
+                pl.BlockSpec(memory_space=pltpu.HBM),
+                pl.BlockSpec(memory_space=pltpu.HBM),
             ],
             out_specs=(pl.BlockSpec(memory_space=pltpu.VMEM), pl.BlockSpec(memory_space=pltpu.VMEM)),
             scratch_shapes=[
+                pltpu.VMEM((rows, feats), hidden.dtype),
+                pltpu.VMEM((feats,), jnp.float32),
                 pltpu.VMEM((SLOTS, feats, CHUNK), jnp.bfloat16),
                 pltpu.VMEM((SLOTS, feats, CHUNK), jnp.bfloat16),
                 pltpu.VMEM((rows, feats), jnp.bfloat16),
@@ -254,6 +272,7 @@
                 pltpu.VMEM((4, 1, LANES), jnp.float32),
                 pltpu.VMEM((16, 1, LANES), jnp.float32),
                 *[pltpu.VMEM((rows, LANES), jnp.float32) for _ in range(3)],
+                dma, dma, pltpu.SemaphoreType.REGULAR((3,)),
                 dma((SLOTS,)), dma((SLOTS,)), dma((4,)), dma((4,)),
                 dma, dma, dma, dma((count,)), dma((count,)), dma((count,)), dma((16,)), dma((16,)),
             ],
@@ -261,7 +280,7 @@
                 collective_id=0, has_side_effects=True, vmem_limit_bytes=48 * 1024 * 1024
             ),
             name="head",
-        )(hidden, norm_gain.reshape(1, feats), w_head)
+        )(pltpu.with_memory_space_constraint(hidden, pltpu.HBM), pltpu.with_memory_space_constraint(norm_gain, pltpu.HBM), w_head)
         log_norm = lse[0, :rows]
         return z - log_norm[:, None], log_norm
 

time: 73.2 us -> 76.6 us (1.046)
  Pallas kernels: 69.1 us -> 74.1 us
  local copies, waits for them, and re-layouts: 1.6 us -> 0.01 us
    pallas_call x1, Pallas kernels: 69.1 us -> 74.1 us  [local_head(): pl.pallas_call(body, out_shape=(jax.ShapeDtypeStruct((rows, width), jnp.f...]
    unnamed x4 -> x2, local copies, waits for them, and re-layouts: 0.9 us -> 0.01 us
where the time goes in v2:
time: 76.6 us; the launch traced here: 76.5 us
  Pallas kernels  74.1 us (97%)
  other arithmetic  1.67 us (2%)
    pallas_call x1, Pallas kernels, local_head(): pl.pallas_call(body, out_shape=(jax.ShapeDtypeStruct((rows, width), jnp.f...  74.1 us
    sub x1, other arithmetic, local_head(): return (z - log_norm[:, None], log_norm)  1.67 us

profile of v2, /device:TPU:0, one launch (start us, length us, event | category | flops | bytes accessed | tf_op | source)
XLA Modules:
  0.0 76.5 jit_solution(3443213331380081244)
XLA Ops:
  0.6 74.1 %head.1 = (f32[64,9504]{1,0:T(8,128)S(1)}, f32[1,128]{1,0:T(1,128)S(1)}) custom-call(bf16[64,896]{1,0:T(8,128)(2,1)} %refs_0_.1, f32[896]{0:T(1024)} %refs_1_.1, bf16[896,38016]{1,0:T(8,128)(2,1)} %refs_2_.1), custom_call_target="tpu_custom_call" | custom-call | tf_op jit(solution)/shard_map/head/pallas_call | solution.py:253
  74.8 0.0 copy-start
  74.8 1.7 %broadcast_subtract_fusion = f32[64,9504]{1,0:T(8,128)} fusion(f32[64,9504]{1,0:T(8,128)S(1)} %get-tuple-element.4, f32[64]{0:T(128)S(1)} %slice_bitcast_fusion), kind=kLoop, calls=%fused_computation | loop fusion | flops 608256 | bytes 4866304 | tf_op jit(solution)/shard_map/sub | solution.py:285
  76.5 0.0 copy-done
  (1 shorter events, 0.0 us)
Async XLA Ops:
  74.8 1.7 %copy-start = (f32[64]{0:T(128)}, f32[64]{0:T(128)S(1)}, u32[]{:S(2)}) copy-start(f32[64]{0:T(128)S(1)} %slice_bitcast_fusion) | copy-start | bytes 772

commit v3 on v2

--- a/solution.py
+++ b/solution.py
@@ -10,6 +10,7 @@
 LANES = 128
 TILES = 3
 CHUNK = TILES * LANES
+EARLY = 2
 SLOTS = 12
 
 
@@ -57,10 +58,10 @@
     g_copy = pltpu.make_async_copy(g_hbm, g_ref, g_sem)
     h_copy.start()
     g_copy.start()
-    for t in range(SLOTS):
+    h_copy.wait()
+    for t in range(EARLY):
         fetch(0, t).start()
         fetch(1, t).start()
-    h_copy.wait()
 
     lane = lax.broadcasted_iota(jnp.int32, (rows, LANES), 1)
     sq = jnp.zeros((rows, LANES), jnp.float32)
@@ -77,8 +78,11 @@
             device_id={"row": lax.rem(row + k, 4)}, device_id_type=MESH,
         )
 
-    for k in range(1, 4):
+    for k in (2, 3, 1):
         norm_copy(k).start()
+    for t in range(EARLY, SLOTS):
+        fetch(0, t).start()
+        fetch(1, t).start()
     for k in range(1, 4):
         peer = lax.rem(row + k, 4)
         pltpu.make_async_remote_copy(
@@ -201,23 +205,23 @@
     me = col * 4 + row
     fst[me] = jnp.where(lane[:1] < rows, peak, mass)
 
-    def stat_copy(dc, dr):
-        k = dc * 4 + dr
-        return pltpu.make_async_remote_copy(
-            src_ref=fst.at[me], dst_ref=fst.at[me], send_sem=fsend.at[k], recv_sem=frecv.at[me],
-            device_id={"col": lax.rem(col + dc, 4), "row": lax.rem(row + dr, 4)}, device_id_type=MESH,
-        )
-
-    peers = [(dc, dr) for dc in (3, 2, 1, 0) for dr in (2, 3, 1, 0) if dc or dr]
-    for dc, dr in peers:
-        stat_copy(dc, dr).start()
-    for dc, dr in peers:
-        pc, pr = lax.rem(col + dc, 4), lax.rem(row + dr, 4)
-        peer = pc * 4 + pr
-        pltpu.make_async_remote_copy(
-            src_ref=fst.at[peer], dst_ref=fst.at[peer], send_sem=fsend.at[dc * 4 + dr], recv_sem=frecv.at[peer],
-            device_id={"col": pc, "row": pr}, device_id_type=MESH,
-        ).wait_recv()
+    peers = [
+        (c, lax.rem(row + dr, 4))
+        for c in (3 - col, lax.rem(col + 2, 4), lax.rem(5 - col, 4), col) for dr in (2, 3, 1, 0)
+    ][:-1]
+
+    def stat_copy(k, slot):
+        c, r = peers[k]
+        return pltpu.make_async_remote_copy(
+            src_ref=fst.at[slot], dst_ref=fst.at[slot], send_sem=fsend.at[k], recv_sem=frecv.at[slot],
+            device_id={"col": c, "row": r}, device_id_type=MESH,
+        )
+
+    for k in range(15):
+        stat_copy(k, me).start()
+    for k in reversed(range(15)):
+        c, r = peers[k]
+        stat_copy(k, c * 4 + r).wait_recv()
     stats = fst[...]
     swapped = pltpu.roll(stats, LANES // 2, 2)
     peak = jnp.max(stats, axis=0)
@@ -235,8 +239,8 @@
         src_ref=rbuf, dst_ref=yin, send_sem=ysend, recv_sem=yrecv.at[0],
         device_id={"row": across}, device_id_type=MESH,
     ).wait_send()
-    for dc, dr in peers:
-        stat_copy(dc, dr).wait_send()
+    for k in range(15):
+        stat_copy(k, me).wait_send()
 
 
 def solution(mesh):

time: 76.6 us -> 71.9 us (0.939)
  Pallas kernels: 74.1 us -> 69.4 us
    pallas_call x1, Pallas kernels: 74.1 us -> 69.4 us  [local_head(): pl.pallas_call(body, out_shape=(jax.ShapeDtypeStruct((rows, width), jnp.f...]
where the time goes in v3:
time: 71.9 us; the launch traced here: 71.7 us
  Pallas kernels  69.4 us (97%)
  other arithmetic  1.67 us (2%)
    pallas_call x1, Pallas kernels, local_head(): pl.pallas_call(body, out_shape=(jax.ShapeDtypeStruct((rows, width), jnp.f...  69.4 us
    sub x1, other arithmetic, local_head(): return (z - log_norm[:, None], log_norm)  1.67 us

profile of v3, /device:TPU:0, one launch (start us, length us, event | category | flops | bytes accessed | tf_op | source)
XLA Modules:
  0.0 71.7 jit_solution(11124245735978727877)
XLA Ops:
  0.6 69.4 %head.1 = (f32[64,9504]{1,0:T(8,128)S(1)}, f32[1,128]{1,0:T(1,128)S(1)}) custom-call(bf16[64,896]{1,0:T(8,128)(2,1)} %refs_0_.1, f32[896]{0:T(1024)} %refs_1_.1, bf16[896,38016]{1,0:T(8,128)(2,1)} %refs_2_.1), custom_call_target="tpu_custom_call" | custom-call | tf_op jit(solution)/shard_map/head/pallas_call | solution.py:257
  70.1 0.0 copy-start
  70.1 1.7 %broadcast_subtract_fusion = f32[64,9504]{1,0:T(8,128)} fusion(f32[64,9504]{1,0:T(8,128)S(1)} %get-tuple-element.4, f32[64]{0:T(128)S(1)} %slice_bitcast_fusion), kind=kLoop, calls=%fused_computation | loop fusion | flops 608256 | bytes 4866304 | tf_op jit(solution)/shard_map/sub | solution.py:289
  71.7 0.0 copy-done
  (1 shorter events, 0.0 us)
Async XLA Ops:
  70.1 1.7 %copy-start = (f32[64]{0:T(128)}, f32[64]{0:T(128)S(1)}, u32[]{:S(2)}) copy-start(f32[64]{0:T(128)S(1)} %slice_bitcast_fusion) | copy-start | bytes 772

commit v4 on v3

--- a/solution.py
+++ b/solution.py
@@ -11,7 +11,7 @@
 TILES = 3
 CHUNK = TILES * LANES
 EARLY = 2
-SLOTS = 12
+SLOTS = 4
 
 
 def head_kernel(

time: 71.9 us -> 71.8 us (level)
  no operation moved by 1% of the time
where the time goes in v4:
time: 71.8 us; the launch traced here: 71.6 us
  Pallas kernels  69.3 us (97%)
  other arithmetic  1.67 us (2%)
    pallas_call x1, Pallas kernels, local_head(): pl.pallas_call(body, out_shape=(jax.ShapeDtypeStruct((rows, width), jnp.f...  69.3 us
    sub x1, other arithmetic, local_head(): return (z - log_norm[:, None], log_norm)  1.67 us

profile of v4, /device:TPU:0, one launch (start us, length us, event | category | flops | bytes accessed | tf_op | source)
XLA Modules:
  0.0 71.6 jit_solution(5562897420116337438)
XLA Ops:
  0.6 69.3 %head.1 = (f32[64,9504]{1,0:T(8,128)S(1)}, f32[1,128]{1,0:T(1,128)S(1)}) custom-call(bf16[64,896]{1,0:T(8,128)(2,1)} %refs_0_.1, f32[896]{0:T(1024)} %refs_1_.1, bf16[896,38016]{1,0:T(8,128)(2,1)} %refs_2_.1), custom_call_target="tpu_custom_call" | custom-call | tf_op jit(solution)/shard_map/head/pallas_call | solution.py:257
  69.9 0.0 copy-start
  69.9 1.7 %broadcast_subtract_fusion = f32[64,9504]{1,0:T(8,128)} fusion(f32[64,9504]{1,0:T(8,128)S(1)} %get-tuple-element.4, f32[64]{0:T(128)S(1)} %slice_bitcast_fusion), kind=kLoop, calls=%fused_computation | loop fusion | flops 608256 | bytes 4866304 | tf_op jit(solution)/shard_map/sub | solution.py:289
  71.6 0.0 copy-done
  (1 shorter events, 0.0 us)
Async XLA Ops:
  69.9 1.7 %copy-start = (f32[64]{0:T(128)}, f32[64]{0:T(128)S(1)}, u32[]{:S(2)}) copy-start(f32[64]{0:T(128)S(1)} %slice_bitcast_fusion) | copy-start | bytes 772

commit v5 on v4

--- a/solution.py
+++ b/solution.py
@@ -8,7 +8,7 @@
 EPS = 1e-5
 MESH = pl.DeviceIdType.MESH
 LANES = 128
-TILES = 3
+TILES = 5
 CHUNK = TILES * LANES
 EARLY = 2
 SLOTS = 4

time: 71.8 us -> 71.8 us (level)
  no operation moved by 1% of the time
where the time goes in v5:
time: 71.8 us; the launch traced here: 71.6 us
  Pallas kernels  69.3 us (97%)
  other arithmetic  1.67 us (2%)
    pallas_call x1, Pallas kernels, local_head(): pl.pallas_call(body, out_shape=(jax.ShapeDtypeStruct((rows, width), jnp.f...  69.3 us
    sub x1, other arithmetic, local_head(): return (z - log_norm[:, None], log_norm)  1.67 us

profile of v5, /device:TPU:0, one launch (start us, length us, event | category | flops | bytes accessed | tf_op | source)
XLA Modules:
  0.0 71.6 jit_solution(5648963540254444164)
XLA Ops:
  0.6 69.3 %head.1 = (f32[64,9504]{1,0:T(8,128)S(1)}, f32[1,128]{1,0:T(1,128)S(1)}) custom-call(bf16[64,896]{1,0:T(8,128)(2,1)} %refs_0_.1, f32[896]{0:T(1024)} %refs_1_.1, bf16[896,38016]{1,0:T(8,128)(2,1)} %refs_2_.1), custom_call_target="tpu_custom_call" | custom-call | tf_op jit(solution)/shard_map/head/pallas_call | solution.py:257
  69.9 0.0 copy-start
  69.9 1.7 %broadcast_subtract_fusion = f32[64,9504]{1,0:T(8,128)} fusion(f32[64,9504]{1,0:T(8,128)S(1)} %get-tuple-element.4, f32[64]{0:T(128)S(1)} %slice_bitcast_fusion), kind=kLoop, calls=%fused_computation | loop fusion | flops 608256 | bytes 4866304 | tf_op jit(solution)/shard_map/sub | solution.py:289
  71.6 0.0 copy-done
  (1 shorter events, 0.0 us)
Async XLA Ops:
  69.9 1.7 %copy-start = (f32[64]{0:T(128)}, f32[64]{0:T(128)S(1)}, u32[]{:S(2)}) copy-start(f32[64]{0:T(128)S(1)} %slice_bitcast_fusion) | copy-start | bytes 772

commit v6 on v4

--- a/solution.py
+++ b/solution.py
@@ -241,6 +241,19 @@
     ).wait_send()
     for k in range(15):
         stat_copy(k, me).wait_send()
+
+
+def finish_kernel(z_ref, lse_ref, out_ref, buf, sems):
+    rows = z_ref.shape[0]
+    column = jnp.transpose(jnp.broadcast_to(lse_ref[...], (LANES, LANES)))[:rows, :1]
+    copies = []
+    for k in range(rows // 8):
+        part = slice(k * 8, k * 8 + 8)
+        buf[part] = z_ref[part] - column[part]
+        copies.append(pltpu.make_async_copy(buf.at[part], out_ref.at[part], sems.at[k]))
+        copies[-1].start()
+    for copy in copies:
+        copy.wait()
 
 
 def solution(mesh):
@@ -286,7 +299,16 @@
             name="head",
         )(pltpu.with_memory_space_constraint(hidden, pltpu.HBM), pltpu.with_memory_space_constraint(norm_gain, pltpu.HBM), w_head)
         log_norm = lse[0, :rows]
-        return z - log_norm[:, None], log_norm
+        log_probs = pl.pallas_call(
+            finish_kernel,
+            out_shape=jax.ShapeDtypeStruct((rows, width), jnp.float32),
+            in_specs=[pl.BlockSpec(memory_space=pltpu.VMEM), pl.BlockSpec(memory_space=pltpu.VMEM)],
+            out_specs=pl.BlockSpec(memory_space=pltpu.HBM),
+            scratch_shapes=[pltpu.VMEM((rows, width), jnp.float32), dma((rows // 8,))],
+            compiler_params=pltpu.CompilerParams(vmem_limit_bytes=8 * 1024 * 1024),
+            name="finish",
+        )(z, lse)
+        return log_probs, log_norm
 
     return jax.shard_map(
         local_head,

time: 71.8 us -> 72.2 us (level)
  other arithmetic: 1.67 us -> 0 us
  Pallas kernels: 69.3 us -> 70.9 us
    sub x1 -> x0, other arithmetic: 1.67 us -> none  [local_head(): return (z - log_norm[:, None], log_norm)]
    pallas_call x0 -> x1, Pallas kernels: none -> 1.65 us  [local_head(): pl.pallas_call(finish_kernel, out_shape=jax.ShapeDtypeStruct((rows, width...]
where the time goes in v6:
time: 72.2 us; the launch traced here: 72.1 us
  Pallas kernels  70.9 us (98%)
    pallas_call x1, Pallas kernels, local_head(): pl.pallas_call(body, out_shape=(jax.ShapeDtypeStruct((rows, width), jnp.f...  69.3 us
    pallas_call x1, Pallas kernels, local_head(): pl.pallas_call(finish_kernel, out_shape=jax.ShapeDtypeStruct((rows, width...  1.65 us

profile of v6, /device:TPU:0, one launch (start us, length us, event | category | flops | bytes accessed | tf_op | source)
XLA Modules:
  0.0 72.1 jit_solution(17474482521079583646)
XLA Ops:
  0.6 69.3 %head.1 = (f32[64,9504]{1,0:T(8,128)S(1)}, f32[1,128]{1,0:T(1,128)S(1)}) custom-call(bf16[64,896]{1,0:T(8,128)(2,1)} %refs_0_.1, f32[896]{0:T(1024)} %refs_1_.1, bf16[896,38016]{1,0:T(8,128)(2,1)} %refs_2_.1), custom_call_target="tpu_custom_call" | custom-call | tf_op jit(solution)/shard_map/head/pallas_call | solution.py:270
  69.9 1.7 %finish.1 = f32[64,9504]{1,0:T(8,128)} custom-call(f32[64,9504]{1,0:T(8,128)S(1)} %get-tuple-element.4.z_ref, f32[1,128]{1,0:T(1,128)S(1)} %get-tuple-element.5.lse_ref), custom_call_target="tpu_custom_call" | custom-call | tf_op jit(solution)/shard_map/finish/pallas_call | solution.py:302
  71.6 0.5 slice_bitcast_fusion

commit v7 on v4

--- a/solution.py
+++ b/solution.py
@@ -11,14 +11,15 @@
 TILES = 3
 CHUNK = TILES * LANES
 EARLY = 2
+GROUPS = (1, 1, 2, 4, 6, 6, 3, 1, 1)
 SLOTS = 4
 
 
 def head_kernel(
     count, width, hidden_size,
     h_hbm, g_hbm, w_ref, z_ref, lse_ref,
-    h_ref, g_ref, wa, wb, x_ref, qbuf, rbuf, pbuf, lbuf, rin, lin, yin, nst, fst, m_ref, s_ref, carry,
-    h_sem, g_sem, hops, wa_sem, wb_sem, nsend, nrecv, qsend, psend, ysend, rrecv, lrecv, yrecv, fsend, frecv,
+    h_ref, g_ref, wa, wb, x_ref, qbuf, rbuf, pbuf, lbuf, rin, lin, yin, nst, fst, m_ref, s_ref, carry, edge_out, edge_in,
+    h_sem, g_sem, hops, wa_sem, wb_sem, nsend, nrecv, qsend, psend, ysend, rrecv, lrecv, yrecv, fsend, frecv, esend, erecv,
 ):
     rows, feats = h_ref.shape
     stride = (width // LANES) * LANES
@@ -115,11 +116,32 @@
             device_id={"row": mate}, device_id_type=MESH,
         )
 
-    def across_copy(i):
+    starts = [sum(GROUPS[:k]) for k in range(len(GROUPS))]
+
+    def across_copy(k, tiles=TILES):
+        part = (pl.ds(starts[k], GROUPS[k]), slice(None), pl.ds(0, tiles * LANES))
         return pltpu.make_async_remote_copy(
-            src_ref=rbuf.at[i], dst_ref=yin.at[i], send_sem=ysend, recv_sem=yrecv.at[i],
+            src_ref=rbuf.at[part], dst_ref=yin.at[part], send_sem=ysend.at[k], recv_sem=yrecv.at[k],
             device_id={"row": across}, device_id_type=MESH,
         )
+
+    def each_across(k, act):
+        if k < len(GROUPS) - 1:
+            act(across_copy(k))
+            return
+
+        @pl.when(core == 0)
+        def _():
+            act(across_copy(k, TILES - 1))
+
+        @pl.when(core == 1)
+        def _():
+            act(across_copy(k))
+
+    edge_copy = pltpu.make_async_remote_copy(
+        src_ref=edge_out, dst_ref=edge_in, send_sem=esend, recv_sem=erecv,
+        device_id={"row": mate}, device_id_type=MESH,
+    )
 
     def far_step(i):
         qbuf[i] = product(0, i)
@@ -131,7 +153,6 @@
         refill(1, i)
         mate_copy(qbuf, rin, qsend, rrecv, i).wait_recv()
         rbuf[i] = term + rin[i]
-        across_copy(i).start()
 
     far_step(0)
 
@@ -139,8 +160,13 @@
     def _(i):
         far_step(i + 1)
         across_step(i)
+        for k in range(len(GROUPS) - 1):
+            @pl.when(i == starts[k] + GROUPS[k] - 1)
+            def _():
+                each_across(k, lambda copy: copy.start())
 
     across_step(count - 1)
+    each_across(len(GROUPS) - 1, lambda copy: copy.start())
     pl.semaphore_wait(hops.at[0], beside)
     tell_columns(hops.at[1])
 
@@ -158,14 +184,30 @@
     turn = lax.rem(LANES - shift, LANES)
     keep = lane < LANES - shift
 
-    def turned(i):
+    def arrive(i, first, last):
         mate_copy(pbuf, lin, psend, lrecv, i).wait_recv()
-        across_copy(i).wait_recv()
+        if first or last:
+            each_across(0 if first else len(GROUPS) - 1, lambda copy: copy.wait_recv())
+        else:
+            for k in range(1, len(GROUPS) - 1):
+                @pl.when(i == starts[k])
+                def _():
+                    each_across(k, lambda copy: copy.wait_recv())
         full = lbuf[i] + lin[i] + yin[i]
-        return [pltpu.roll(full[:, k * LANES:(k + 1) * LANES], turn, 1) for k in range(TILES)]
-
-    def arrive(i, first):
-        rolled = turned(i)
+        parts = [full[:, k * LANES:(k + 1) * LANES] for k in range(TILES)]
+        if first:
+            edge_out[...] = parts[0]
+
+            @pl.when(core == 1)
+            def _():
+                edge_copy.start()
+        if last:
+            @pl.when(core == 0)
+            def _():
+                edge_copy.wait_recv()
+
+            parts[-1] = jnp.where(core == 0, edge_in[...], parts[-1])
+        rolled = [pltpu.roll(part, turn, 1) for part in parts]
         tiles = [jnp.where(keep, rolled[k], rolled[k + 1]) for k in range(TILES - 1)]
         at = 0
         if not first:
@@ -186,12 +228,14 @@
         m_ref[...] = top
         s_ref[...] = mass
 
-    arrive(0, True)
+    arrive(0, True, False)
     pl.semaphore_wait(hops.at[2], beside)
 
-    @pl.loop(1, count)
+    @pl.loop(1, count - 1)
     def _(i):
-        arrive(i, False)
+        arrive(i, False, False)
+
+    arrive(count - 1, False, True)
 
     last = carry[...]
     z_ref[:, stride:] = last[:, :rest]
@@ -235,10 +279,13 @@
             src_ref=src, dst_ref=dst, send_sem=send, recv_sem=recv.at[0],
             device_id={"row": mate}, device_id_type=MESH,
         ).wait_send()
-    pltpu.make_async_remote_copy(
-        src_ref=rbuf, dst_ref=yin, send_sem=ysend, recv_sem=yrecv.at[0],
-        device_id={"row": across}, device_id_type=MESH,
-    ).wait_send()
+    for k in range(len(GROUPS)):
+        each_across(k, lambda copy: copy.wait_send())
+
+    @pl.when(core == 1)
+    def _():
+        edge_copy.wait_send()
+
     for k in range(15):
         stat_copy(k, me).wait_send()
 
@@ -275,10 +322,10 @@
                 *[pltpu.VMEM(block, jnp.float32) for _ in range(7)],
                 pltpu.VMEM((4, 1, LANES), jnp.float32),
                 pltpu.VMEM((16, 1, LANES), jnp.float32),
-                *[pltpu.VMEM((rows, LANES), jnp.float32) for _ in range(3)],
+                *[pltpu.VMEM((rows, LANES), jnp.float32) for _ in range(5)],
                 dma, dma, pltpu.SemaphoreType.REGULAR((3,)),
                 dma((SLOTS,)), dma((SLOTS,)), dma((4,)), dma((4,)),
-                dma, dma, dma, dma((count,)), dma((count,)), dma((count,)), dma((16,)), dma((16,)),
+                dma, dma, dma((len(GROUPS),)), dma((count,)), dma((count,)), dma((len(GROUPS),)), dma((16,)), dma((16,)), dma, dma,
             ],
             compiler_params=pltpu.CompilerParams(
                 collective_id=0, has_side_effects=True, vmem_limit_bytes=48 * 1024 * 1024

time: 71.8 us -> 71 us (0.989)
  Pallas kernels: 69.3 us -> 68.5 us
    pallas_call x1, Pallas kernels: 69.3 us -> 68.5 us  [local_head(): pl.pallas_call(body, out_shape=(jax.ShapeDtypeStruct((rows, width), jnp.f...]
where the time goes in v7:
time: 71 us; the launch traced here: 70.9 us
  Pallas kernels  68.5 us (96%)
  other arithmetic  1.67 us (2%)
    pallas_call x1, Pallas kernels, local_head(): pl.pallas_call(body, out_shape=(jax.ShapeDtypeStruct((rows, width), jnp.f...  68.5 us
    sub x1, other arithmetic, local_head(): return (z - log_norm[:, None], log_norm)  1.67 us

profile of v7, /device:TPU:0, one launch (start us, length us, event | category | flops | bytes accessed | tf_op | source)
XLA Modules:
  0.0 70.9 jit_solution(13869398799665572546)
XLA Ops:
  0.6 68.5 %head.1 = (f32[64,9504]{1,0:T(8,128)S(1)}, f32[1,128]{1,0:T(1,128)S(1)}) custom-call(bf16[64,896]{1,0:T(8,128)(2,1)} %refs_0_.1, f32[896]{0:T(1024)} %refs_1_.1, bf16[896,38016]{1,0:T(8,128)(2,1)} %refs_2_.1), custom_call_target="tpu_custom_call" | custom-call | tf_op jit(solution)/shard_map/head/pallas_call | solution.py:304
  69.2 0.0 copy-start
  69.2 1.7 %broadcast_subtract_fusion = f32[64,9504]{1,0:T(8,128)} fusion(f32[64,9504]{1,0:T(8,128)S(1)} %get-tuple-element.4, f32[64]{0:T(128)S(1)} %slice_bitcast_fusion), kind=kLoop, calls=%fused_computation | loop fusion | flops 608256 | bytes 4866304 | tf_op jit(solution)/shard_map/sub | solution.py:336
  70.9 0.0 copy-done
  (1 shorter events, 0.0 us)
Async XLA Ops:
  69.2 1.7 %copy-start = (f32[64]{0:T(128)}, f32[64]{0:T(128)S(1)}, u32[]{:S(2)}) copy-start(f32[64]{0:T(128)S(1)} %slice_bitcast_fusion) | copy-start | bytes 772

commit v8 on v7

--- a/solution.py
+++ b/solution.py
@@ -11,15 +11,16 @@
 TILES = 3
 CHUNK = TILES * LANES
 EARLY = 2
-GROUPS = (1, 1, 2, 4, 6, 6, 3, 1, 1)
+GROUPS = (1, 1, 2, 4, 6, 6, 3, 1)
+RELAY_AT = 10
 SLOTS = 4
 
 
 def head_kernel(
     count, width, hidden_size,
     h_hbm, g_hbm, w_ref, z_ref, lse_ref,
-    h_ref, g_ref, wa, wb, x_ref, qbuf, rbuf, pbuf, lbuf, rin, lin, yin, nst, fst, m_ref, s_ref, carry, edge_out, edge_in,
-    h_sem, g_sem, hops, wa_sem, wb_sem, nsend, nrecv, qsend, psend, ysend, rrecv, lrecv, yrecv, fsend, frecv, esend, erecv,
+    h_ref, g_ref, wa, wb, x_ref, qbuf, rbuf, pbuf, lbuf, rin, lin, yin, nst, fst, m_ref, s_ref, carry, edge_out, edge_in, relay_in, relay_mid,
+    h_sem, g_sem, hops, wa_sem, wb_sem, nsend, nrecv, qsend, psend, ysend, rrecv, lrecv, yrecv, fsend, frecv, esend, erecv, tail_send, tail_recv, relay_send, relay_recv,
 ):
     rows, feats = h_ref.shape
     stride = (width // LANES) * LANES
@@ -32,13 +33,20 @@
     far = 3 - row
     shift = row * rest
 
+    end = count - 1
+
+    def chunk_at(t):
+        if isinstance(t, int) and t < 2:
+            return t * end
+        return t - 1 - end * (t // count)
+
     def fetch(stream, t):
         if stream == 0:
             first, second, buf, sem = far, mate, wa, wa_sem
         else:
             first, second, buf, sem = across, row, wb, wb_sem
         part = first + (second - first) * (t // count)
-        start = pl.multiple_of(stride * part + CHUNK * lax.rem(t, count), LANES)
+        start = pl.multiple_of(stride * part + CHUNK * chunk_at(t), LANES)
         slot = lax.rem(t, SLOTS)
         return pltpu.make_async_copy(w_ref.at[:, pl.ds(start, CHUNK)], buf.at[slot], sem.at[slot])
 
@@ -72,6 +80,7 @@
     sq = jnp.transpose(jnp.concatenate([sq, sq], axis=0))
     nst[row] = jnp.sum(sq, axis=0, keepdims=True)
     pl.semaphore_wait(barrier, 3 + beside)
+    tell_columns(hops.at[0])
 
     def norm_copy(k):
         return pltpu.make_async_remote_copy(
@@ -90,7 +99,6 @@
             src_ref=nst.at[peer], dst_ref=nst.at[peer], send_sem=nsend.at[k], recv_sem=nrecv.at[peer],
             device_id={"row": peer}, device_id_type=MESH,
         ).wait_recv()
-    tell_columns(hops.at[0])
     g_copy.wait()
     total = nst[0] + nst[1] + nst[2] + nst[3]
     scale = lax.rsqrt(total / hidden_size + EPS)
@@ -118,57 +126,93 @@
 
     starts = [sum(GROUPS[:k]) for k in range(len(GROUPS))]
 
-    def across_copy(k, tiles=TILES):
-        part = (pl.ds(starts[k], GROUPS[k]), slice(None), pl.ds(0, tiles * LANES))
+    def across_copy(k):
+        part = pl.ds(starts[k], GROUPS[k])
         return pltpu.make_async_remote_copy(
             src_ref=rbuf.at[part], dst_ref=yin.at[part], send_sem=ysend.at[k], recv_sem=yrecv.at[k],
             device_id={"row": across}, device_id_type=MESH,
         )
 
-    def each_across(k, act):
-        if k < len(GROUPS) - 1:
-            act(across_copy(k))
-            return
-
-        @pl.when(core == 0)
-        def _():
-            act(across_copy(k, TILES - 1))
-
-        @pl.when(core == 1)
-        def _():
-            act(across_copy(k))
+    most = pl.ds(0, (TILES - 1) * LANES)
+
+    def tail_copy(lanes):
+        return pltpu.make_async_remote_copy(
+            src_ref=rbuf.at[end, :, lanes], dst_ref=yin.at[end, :, lanes], send_sem=tail_send, recv_sem=tail_recv,
+            device_id={"row": across}, device_id_type=MESH,
+        )
+
+    def each_tail(act):
+        @pl.when((col < 3) & (core == 0))
+        def _():
+            act(tail_copy(most))
+
+        @pl.when((col < 3) & (core == 1))
+        def _():
+            act(tail_copy(pl.ds(0, CHUNK)))
+
+        @pl.when((col == 3) & (core == 1))
+        def _():
+            act(tail_copy(pl.ds((TILES - 1) * LANES, LANES)))
+
+    def relay_copy(k):
+        src, dst, device = (
+            (rbuf.at[end, :, most], relay_in, {"col": 0}),
+            (relay_in, relay_mid, {"row": across}),
+            (relay_mid, yin.at[end, :, most], {"col": 3}),
+        )[k]
+        return pltpu.make_async_remote_copy(
+            src_ref=src, dst_ref=dst, send_sem=relay_send.at[k], recv_sem=relay_recv.at[k],
+            device_id=device, device_id_type=MESH,
+        )
 
     edge_copy = pltpu.make_async_remote_copy(
         src_ref=edge_out, dst_ref=edge_in, send_sem=esend, recv_sem=erecv,
         device_id={"row": mate}, device_id_type=MESH,
     )
 
-    def far_step(i):
-        qbuf[i] = product(0, i)
+    def far_step(t, i):
+        qbuf[i] = product(0, t)
         mate_copy(qbuf, rin, qsend, rrecv, i).start()
-        refill(0, i)
-
-    def across_step(i):
-        term = product(1, i)
-        refill(1, i)
+        refill(0, t)
+
+    def across_step(t, i):
+        term = product(1, t)
+        refill(1, t)
         mate_copy(qbuf, rin, qsend, rrecv, i).wait_recv()
         rbuf[i] = term + rin[i]
 
-    far_step(0)
-
-    @pl.loop(0, count - 1)
-    def _(i):
-        far_step(i + 1)
-        across_step(i)
-        for k in range(len(GROUPS) - 1):
-            @pl.when(i == starts[k] + GROUPS[k] - 1)
-            def _():
-                each_across(k, lambda copy: copy.start())
-
-    across_step(count - 1)
-    each_across(len(GROUPS) - 1, lambda copy: copy.start())
     pl.semaphore_wait(hops.at[0], beside)
     tell_columns(hops.at[1])
+    far_step(0, 0)
+    far_step(1, end)
+    across_step(0, 0)
+    across_copy(0).start()
+    far_step(2, 1)
+    across_step(1, end)
+    pl.semaphore_wait(hops.at[1], beside)
+    tell_columns(hops.at[2])
+    each_tail(lambda copy: copy.start())
+
+    @pl.when(col == 3)
+    def _():
+        relay_copy(0).start()
+
+    @pl.loop(2, count)
+    def _(t):
+        @pl.when(t < end)
+        def _():
+            far_step(t + 1, t)
+
+        across_step(t, t - 1)
+        for k in range(1, len(GROUPS)):
+            @pl.when(t == starts[k] + GROUPS[k])
+            def _():
+                across_copy(k).start()
+
+        @pl.when((t == RELAY_AT) & (col == 0))
+        def _():
+            relay_copy(0).wait_recv()
+            relay_copy(1).start()
 
     @pl.loop(0, count)
     def _(i):
@@ -178,21 +222,29 @@
         lbuf[i] = product(1, count + i)
         refill(1, count + i)
 
-    pl.semaphore_wait(hops.at[1], beside)
-    tell_columns(hops.at[2])
+    @pl.when(col == 0)
+    def _():
+        relay_copy(1).wait_recv()
+        relay_copy(2).start()
 
     turn = lax.rem(LANES - shift, LANES)
     keep = lane < LANES - shift
 
     def arrive(i, first, last):
         mate_copy(pbuf, lin, psend, lrecv, i).wait_recv()
-        if first or last:
-            each_across(0 if first else len(GROUPS) - 1, lambda copy: copy.wait_recv())
+        if first:
+            across_copy(0).wait_recv()
+        elif last:
+            each_tail(lambda copy: copy.wait_recv())
+
+            @pl.when(col == 3)
+            def _():
+                relay_copy(2).wait_recv()
         else:
-            for k in range(1, len(GROUPS) - 1):
+            for k in range(1, len(GROUPS)):
                 @pl.when(i == starts[k])
                 def _():
-                    each_across(k, lambda copy: copy.wait_recv())
+                    across_copy(k).wait_recv()
         full = lbuf[i] + lin[i] + yin[i]
         parts = [full[:, k * LANES:(k + 1) * LANES] for k in range(TILES)]
         if first:
@@ -280,7 +332,17 @@
             device_id={"row": mate}, device_id_type=MESH,
         ).wait_send()
     for k in range(len(GROUPS)):
-        each_across(k, lambda copy: copy.wait_send())
+        across_copy(k).wait_send()
+    each_tail(lambda copy: copy.wait_send())
+
+    @pl.when(col == 3)
+    def _():
+        relay_copy(0).wait_send()
+
+    @pl.when(col == 0)
+    def _():
+        relay_copy(1).wait_send()
+        relay_copy(2).wait_send()
 
     @pl.when(core == 1)
     def _():
@@ -323,9 +385,10 @@
                 pltpu.VMEM((4, 1, LANES), jnp.float32),
                 pltpu.VMEM((16, 1, LANES), jnp.float32),
                 *[pltpu.VMEM((rows, LANES), jnp.float32) for _ in range(5)],
+                *[pltpu.VMEM((rows, (TILES - 1) * LANES), jnp.float32) for _ in range(2)],
                 dma, dma, pltpu.SemaphoreType.REGULAR((3,)),
                 dma((SLOTS,)), dma((SLOTS,)), dma((4,)), dma((4,)),
-                dma, dma, dma((len(GROUPS),)), dma((count,)), dma((count,)), dma((len(GROUPS),)), dma((16,)), dma((16,)), dma, dma,
+                dma, dma, dma((len(GROUPS),)), dma((count,)), dma((count,)), dma((len(GROUPS),)), dma((16,)), dma((16,)), dma, dma, dma, dma, dma((3,)), dma((3,)),
             ],
             compiler_params=pltpu.CompilerParams(
                 collective_id=0, has_side_effects=True, vmem_limit_bytes=48 * 1024 * 1024

time: 71 us -> 70.8 us (level)
  no operation moved by 1% of the time
where the time goes in v8:
time: 70.8 us; the launch traced here: 70.7 us
  Pallas kernels  68.3 us (96%)
  other arithmetic  1.67 us (2%)
    pallas_call x1, Pallas kernels, local_head(): pl.pallas_call(body, out_shape=(jax.ShapeDtypeStruct((rows, width), jnp.f...  68.3 us
    sub x1, other arithmetic, local_head(): return (z - log_norm[:, None], log_norm)  1.67 us

profile of v8, /device:TPU:0, one launch (start us, length us, event | category | flops | bytes accessed | tf_op | source)
XLA Modules:
  0.0 70.7 jit_solution(5266680278413811380)
XLA Ops:
  0.6 68.3 %head.1 = (f32[64,9504]{1,0:T(8,128)S(1)}, f32[1,128]{1,0:T(1,128)S(1)}) custom-call(bf16[64,896]{1,0:T(8,128)(2,1)} %refs_0_.1, f32[896]{0:T(1024)} %refs_1_.1, bf16[896,38016]{1,0:T(8,128)(2,1)} %refs_2_.1), custom_call_target="tpu_custom_call" | custom-call | tf_op jit(solution)/shard_map/head/pallas_call | solution.py:366
  69.0 0.0 copy-start
  69.0 1.7 %broadcast_subtract_fusion = f32[64,9504]{1,0:T(8,128)} fusion(f32[64,9504]{1,0:T(8,128)S(1)} %get-tuple-element.4, f32[64]{0:T(128)S(1)} %slice_bitcast_fusion), kind=kLoop, calls=%fused_computation | loop fusion | flops 608256 | bytes 4866304 | tf_op jit(solution)/shard_map/sub | solution.py:399
  70.7 0.0 copy-done
  (1 shorter events, 0.0 us)
Async XLA Ops:
  69.0 1.7 %copy-start = (f32[64]{0:T(128)}, f32[64]{0:T(128)S(1)}, u32[]{:S(2)}) copy-start(f32[64]{0:T(128)S(1)} %slice_bitcast_fusion) | copy-start | bytes 772

commit v9 on v8

--- a/solution.py
+++ b/solution.py
@@ -11,9 +11,9 @@
 TILES = 3
 CHUNK = TILES * LANES
 EARLY = 2
-GROUPS = (1, 1, 2, 4, 6, 6, 3, 1)
-RELAY_AT = 10
-SLOTS = 4
+GROUPS = (1, 1, 1, 1, 2, 3, 4, 5, 4, 1, 1)
+RELAY_AT = (16, 18)
+SLOTS = 6
 
 
 def head_kernel(
@@ -188,6 +188,7 @@
     across_step(0, 0)
     across_copy(0).start()
     far_step(2, 1)
+    far_step(3, 2)
     across_step(1, end)
     pl.semaphore_wait(hops.at[1], beside)
     tell_columns(hops.at[2])
@@ -199,9 +200,9 @@
 
     @pl.loop(2, count)
     def _(t):
-        @pl.when(t < end)
-        def _():
-            far_step(t + 1, t)
+        @pl.when(t < end - 1)
+        def _():
+            far_step(t + 2, t + 1)
 
         across_step(t, t - 1)
         for k in range(1, len(GROUPS)):
@@ -209,7 +210,7 @@
             def _():
                 across_copy(k).start()
 
-        @pl.when((t == RELAY_AT) & (col == 0))
+        @pl.when((t == RELAY_AT[0]) & (col == 0))
         def _():
             relay_copy(0).wait_recv()
             relay_copy(1).start()
@@ -221,11 +222,6 @@
         refill(0, count + i)
         lbuf[i] = product(1, count + i)
         refill(1, count + i)
-
-    @pl.when(col == 0)
-    def _():
-        relay_copy(1).wait_recv()
-        relay_copy(2).start()
 
     turn = lax.rem(LANES - shift, LANES)
     keep = lane < LANES - shift
@@ -286,6 +282,11 @@
     @pl.loop(1, count - 1)
     def _(i):
         arrive(i, False, False)
+
+        @pl.when((i == RELAY_AT[1]) & (col == 0))
+        def _():
+            relay_copy(1).wait_recv()
+            relay_copy(2).start()
 
     arrive(count - 1, False, True)
 

time: 70.8 us -> 72.1 us (1.018)
  Pallas kernels: 68.3 us -> 69.7 us
    pallas_call x1, Pallas kernels: 68.3 us -> 69.7 us  [local_head(): pl.pallas_call(body, out_shape=(jax.ShapeDtypeStruct((rows, width), jnp.f...]
where the time goes in v9:
time: 72.1 us; the launch traced here: 72 us
  Pallas kernels  69.7 us (97%)
  other arithmetic  1.67 us (2%)
    pallas_call x1, Pallas kernels, local_head(): pl.pallas_call(body, out_shape=(jax.ShapeDtypeStruct((rows, width), jnp.f...  69.7 us
    sub x1, other arithmetic, local_head(): return (z - log_norm[:, None], log_norm)  1.67 us

profile of v9, /device:TPU:0, one launch (start us, length us, event | category | flops | bytes accessed | tf_op | source)
XLA Modules:
  0.0 72.0 jit_solution(2413194440633938086)
XLA Ops:
  0.6 69.7 %head.1 = (f32[64,9504]{1,0:T(8,128)S(1)}, f32[1,128]{1,0:T(1,128)S(1)}) custom-call(bf16[64,896]{1,0:T(8,128)(2,1)} %refs_0_.1, f32[896]{0:T(1024)} %refs_1_.1, bf16[896,38016]{1,0:T(8,128)(2,1)} %refs_2_.1), custom_call_target="tpu_custom_call" | custom-call | tf_op jit(solution)/shard_map/head/pallas_call | solution.py:367
  70.3 0.0 copy-start
  70.3 1.7 %broadcast_subtract_fusion = f32[64,9504]{1,0:T(8,128)} fusion(f32[64,9504]{1,0:T(8,128)S(1)} %get-tuple-element.4, f32[64]{0:T(128)S(1)} %slice_bitcast_fusion), kind=kLoop, calls=%fused_computation | loop fusion | flops 608256 | bytes 4866304 | tf_op jit(solution)/shard_map/sub | solution.py:400
  72.0 0.0 copy-done
  (1 shorter events, 0.0 us)
Async XLA Ops:
  70.3 1.7 %copy-start = (f32[64]{0:T(128)}, f32[64]{0:T(128)S(1)}, u32[]{:S(2)}) copy-start(f32[64]{0:T(128)S(1)} %slice_bitcast_fusion) | copy-start | bytes 772

commit v10 on v9

--- a/solution.py
+++ b/solution.py
@@ -10,17 +10,15 @@
 LANES = 128
 TILES = 3
 CHUNK = TILES * LANES
-EARLY = 2
-GROUPS = (1, 1, 1, 1, 2, 3, 4, 5, 4, 1, 1)
-RELAY_AT = (16, 18)
-SLOTS = 6
+SLOTS = 3
+RELAY_AT = (4, 10)
 
 
 def head_kernel(
     count, width, hidden_size,
     h_hbm, g_hbm, w_ref, z_ref, lse_ref,
-    h_ref, g_ref, wa, wb, x_ref, qbuf, rbuf, pbuf, lbuf, rin, lin, yin, nst, fst, m_ref, s_ref, carry, edge_out, edge_in, relay_in, relay_mid,
-    h_sem, g_sem, hops, wa_sem, wb_sem, nsend, nrecv, qsend, psend, ysend, rrecv, lrecv, yrecv, fsend, frecv, esend, erecv, tail_send, tail_recv, relay_send, relay_recv,
+    h_ref, g_ref, wq, wr, wp, wl, x_ref, qbuf, rbuf, pbuf, lbuf, rin, lin, yin, nst, fst, m_ref, s_ref, carry, edge_out, edge_in, relay_in, relay_mid,
+    h_sem, g_sem, hops, wq_sem, wr_sem, wp_sem, wl_sem, nsend, nrecv, qsend, psend, ysend, rrecv, lrecv, yrecv, fsend, frecv, esend, erecv, tail_send, tail_recv, relay_send, relay_recv,
 ):
     rows, feats = h_ref.shape
     stride = (width // LANES) * LANES
@@ -35,18 +33,16 @@
 
     end = count - 1
 
-    def chunk_at(t):
-        if isinstance(t, int) and t < 2:
-            return t * end
-        return t - 1 - end * (t // count)
-
-    def fetch(stream, t):
-        if stream == 0:
-            first, second, buf, sem = far, mate, wa, wa_sem
-        else:
-            first, second, buf, sem = across, row, wb, wb_sem
-        part = first + (second - first) * (t // count)
-        start = pl.multiple_of(stride * part + CHUNK * chunk_at(t), LANES)
+    streams = {
+        "far": (far, wq, wq_sem), "across": (across, wr, wr_sem), "mate": (mate, wp, wp_sem), "own": (row, wl, wl_sem)
+    }
+
+    def fetch(name, t):
+        part, buf, sem = streams[name]
+        chunk = t
+        if name in ("far", "across"):
+            chunk = (0, end)[t] if isinstance(t, int) and t < 2 else t - 1
+        start = pl.multiple_of(stride * part + CHUNK * chunk, LANES)
         slot = lax.rem(t, SLOTS)
         return pltpu.make_async_copy(w_ref.at[:, pl.ds(start, CHUNK)], buf.at[slot], sem.at[slot])
 
@@ -68,9 +64,8 @@
     h_copy.start()
     g_copy.start()
     h_copy.wait()
-    for t in range(EARLY):
-        fetch(0, t).start()
-        fetch(1, t).start()
+    for name, t in (("far", 0), ("far", 1), ("across", 0)):
+        fetch(name, t).start()
 
     lane = lax.broadcasted_iota(jnp.int32, (rows, LANES), 1)
     sq = jnp.zeros((rows, LANES), jnp.float32)
@@ -90,9 +85,8 @@
 
     for k in (2, 3, 1):
         norm_copy(k).start()
-    for t in range(EARLY, SLOTS):
-        fetch(0, t).start()
-        fetch(1, t).start()
+    for name, t in (("far", 2), ("across", 1), ("across", 2), *[(n, t) for t in range(SLOTS) for n in ("mate", "own")]):
+        fetch(name, t).start()
     for k in range(1, 4):
         peer = lax.rem(row + k, 4)
         pltpu.make_async_remote_copy(
@@ -107,16 +101,14 @@
         cols = slice(j * LANES, (j + 1) * LANES)
         x_ref[:, cols] = (h_ref[:, cols].astype(jnp.float32) * scale * g_ref[cols].reshape(1, LANES)).astype(jnp.bfloat16)
 
-    def product(stream, t):
-        buf, sem = ((wa, wa_sem), (wb, wb_sem))[stream]
-        fetch(stream, t).wait()
-        slot = lax.rem(t, SLOTS)
-        return jnp.dot(x_ref[...], buf[slot], preferred_element_type=jnp.float32)
-
-    def refill(stream, t):
-        @pl.when(t + SLOTS < 2 * count)
-        def _():
-            fetch(stream, t + SLOTS).start()
+    def product(name, t):
+        fetch(name, t).wait()
+        return jnp.dot(x_ref[...], streams[name][1][lax.rem(t, SLOTS)], preferred_element_type=jnp.float32)
+
+    def refill(name, t):
+        @pl.when(t + SLOTS < count)
+        def _():
+            fetch(name, t + SLOTS).start()
 
     def mate_copy(src, dst, send, recv, i):
         return pltpu.make_async_remote_copy(
@@ -124,12 +116,9 @@
             device_id={"row": mate}, device_id_type=MESH,
         )
 
-    starts = [sum(GROUPS[:k]) for k in range(len(GROUPS))]
-
-    def across_copy(k):
-        part = pl.ds(starts[k], GROUPS[k])
-        return pltpu.make_async_remote_copy(
-            src_ref=rbuf.at[part], dst_ref=yin.at[part], send_sem=ysend.at[k], recv_sem=yrecv.at[k],
+    def across_copy(i):
+        return pltpu.make_async_remote_copy(
+            src_ref=rbuf.at[i], dst_ref=yin.at[i], send_sem=ysend.at[i], recv_sem=yrecv.at[i],
             device_id={"row": across}, device_id_type=MESH,
         )
 
@@ -171,76 +160,38 @@
     )
 
     def far_step(t, i):
-        qbuf[i] = product(0, t)
+        qbuf[i] = product("far", t)
         mate_copy(qbuf, rin, qsend, rrecv, i).start()
-        refill(0, t)
+        refill("far", t)
 
     def across_step(t, i):
-        term = product(1, t)
-        refill(1, t)
+        term = product("across", t)
+        refill("across", t)
         mate_copy(qbuf, rin, qsend, rrecv, i).wait_recv()
         rbuf[i] = term + rin[i]
 
-    pl.semaphore_wait(hops.at[0], beside)
-    tell_columns(hops.at[1])
-    far_step(0, 0)
-    far_step(1, end)
-    across_step(0, 0)
-    across_copy(0).start()
-    far_step(2, 1)
-    far_step(3, 2)
-    across_step(1, end)
-    pl.semaphore_wait(hops.at[1], beside)
-    tell_columns(hops.at[2])
-    each_tail(lambda copy: copy.start())
-
-    @pl.when(col == 3)
-    def _():
-        relay_copy(0).start()
-
-    @pl.loop(2, count)
-    def _(t):
-        @pl.when(t < end - 1)
-        def _():
-            far_step(t + 2, t + 1)
-
-        across_step(t, t - 1)
-        for k in range(1, len(GROUPS)):
-            @pl.when(t == starts[k] + GROUPS[k])
-            def _():
-                across_copy(k).start()
-
-        @pl.when((t == RELAY_AT[0]) & (col == 0))
-        def _():
-            relay_copy(0).wait_recv()
-            relay_copy(1).start()
-
-    @pl.loop(0, count)
-    def _(i):
-        pbuf[i] = product(0, count + i)
+    def mate_step(i):
+        pbuf[i] = product("mate", i)
         mate_copy(pbuf, lin, psend, lrecv, i).start()
-        refill(0, count + i)
-        lbuf[i] = product(1, count + i)
-        refill(1, count + i)
+        refill("mate", i)
+
+    def own_step(i):
+        lbuf[i] = product("own", i)
+        refill("own", i)
 
     turn = lax.rem(LANES - shift, LANES)
     keep = lane < LANES - shift
 
     def arrive(i, first, last):
         mate_copy(pbuf, lin, psend, lrecv, i).wait_recv()
-        if first:
-            across_copy(0).wait_recv()
-        elif last:
+        if last:
             each_tail(lambda copy: copy.wait_recv())
 
             @pl.when(col == 3)
             def _():
                 relay_copy(2).wait_recv()
         else:
-            for k in range(1, len(GROUPS)):
-                @pl.when(i == starts[k])
-                def _():
-                    across_copy(k).wait_recv()
+            across_copy(i).wait_recv()
         full = lbuf[i] + lin[i] + yin[i]
         parts = [full[:, k * LANES:(k + 1) * LANES] for k in range(TILES)]
         if first:
@@ -276,19 +227,58 @@
         m_ref[...] = top
         s_ref[...] = mass
 
+    pl.semaphore_wait(hops.at[0], beside)
+    tell_columns(hops.at[1])
+    far_step(0, 0)
+    far_step(1, end)
+    across_step(0, 0)
+    across_copy(0).start()
+    far_step(2, 1)
+    far_step(3, 2)
+    across_step(1, end)
+    pl.semaphore_wait(hops.at[1], beside)
+    tell_columns(hops.at[2])
+    each_tail(lambda copy: copy.start())
+
+    @pl.when(col == 3)
+    def _():
+        relay_copy(0).start()
+
+    across_step(2, 1)
+    across_copy(1).start()
+    mate_step(0)
+    mate_step(1)
+    own_step(0)
     arrive(0, True, False)
-    pl.semaphore_wait(hops.at[2], beside)
-
-    @pl.loop(1, count - 1)
+
+    @pl.loop(1, end)
     def _(i):
+        @pl.when(i < end - 2)
+        def _():
+            far_step(i + 3, i + 2)
+
+        @pl.when(i < end - 1)
+        def _():
+            across_step(i + 2, i + 1)
+            across_copy(i + 1).start()
+
+        mate_step(i + 1)
+        own_step(i)
         arrive(i, False, False)
+
+        @pl.when((i == RELAY_AT[0]) & (col == 0))
+        def _():
+            relay_copy(0).wait_recv()
+            relay_copy(1).start()
 
         @pl.when((i == RELAY_AT[1]) & (col == 0))
         def _():
             relay_copy(1).wait_recv()
             relay_copy(2).start()
 
-    arrive(count - 1, False, True)
+    pl.semaphore_wait(hops.at[2], beside)
+    own_step(end)
+    arrive(end, False, True)
 
     last = carry[...]
     z_ref[:, stride:] = last[:, :rest]
@@ -332,8 +322,10 @@
             src_ref=src, dst_ref=dst, send_sem=send, recv_sem=recv.at[0],
             device_id={"row": mate}, device_id_type=MESH,
         ).wait_send()
-    for k in range(len(GROUPS)):
-        across_copy(k).wait_send()
+    @pl.loop(0, end)
+    def _(i):
+        across_copy(i).wait_send()
+
     each_tail(lambda copy: copy.wait_send())
 
     @pl.when(col == 3)
@@ -379,8 +371,7 @@
             scratch_shapes=[
                 pltpu.VMEM((rows, feats), hidden.dtype),
                 pltpu.VMEM((feats,), jnp.float32),
-                pltpu.VMEM((SLOTS, feats, CHUNK), jnp.bfloat16),
-                pltpu.VMEM((SLOTS, feats, CHUNK), jnp.bfloat16),
+                *[pltpu.VMEM((SLOTS, feats, CHUNK), jnp.bfloat16) for _ in range(4)],
                 pltpu.VMEM((rows, feats), jnp.bfloat16),
                 *[pltpu.VMEM(block, jnp.float32) for _ in range(7)],
                 pltpu.VMEM((4, 1, LANES), jnp.float32),
@@ -388,8 +379,8 @@
                 *[pltpu.VMEM((rows, LANES), jnp.float32) for _ in range(5)],
                 *[pltpu.VMEM((rows, (TILES - 1) * LANES), jnp.float32) for _ in range(2)],
                 dma, dma, pltpu.SemaphoreType.REGULAR((3,)),
-                dma((SLOTS,)), dma((SLOTS,)), dma((4,)), dma((4,)),
-                dma, dma, dma((len(GROUPS),)), dma((count,)), dma((count,)), dma((len(GROUPS),)), dma((16,)), dma((16,)), dma, dma, dma, dma, dma((3,)), dma((3,)),
+                *[dma((SLOTS,)) for _ in range(4)], dma((4,)), dma((4,)),
+                dma, dma, dma((count,)), dma((count,)), dma((count,)), dma((count,)), dma((16,)), dma((16,)), dma, dma, dma, dma, dma((3,)), dma((3,)),
             ],
             compiler_params=pltpu.CompilerParams(
                 collective_id=0, has_side_effects=True, vmem_limit_bytes=48 * 1024 * 1024

time: 72.1 us -> 78 us (1.082)
  Pallas kernels: 69.7 us -> 75.6 us
    pallas_call x1, Pallas kernels: 69.7 us -> 75.6 us  [local_head(): pl.pallas_call(body, out_shape=(jax.ShapeDtypeStruct((rows, width), jnp.f...]
where the time goes in v10:
time: 78 us; the launch traced here: 77.9 us
  Pallas kernels  75.6 us (97%)
  other arithmetic  1.67 us (2%)
    pallas_call x1, Pallas kernels, local_head(): pl.pallas_call(body, out_shape=(jax.ShapeDtypeStruct((rows, width), jnp.f...  75.6 us
    sub x1, other arithmetic, local_head(): return (z - log_norm[:, None], log_norm)  1.67 us

profile of v10, /device:TPU:0, one launch (start us, length us, event | category | flops | bytes accessed | tf_op | source)
XLA Modules:
  0.0 77.9 jit_solution(4489983169514075422)
XLA Ops:
  0.6 75.6 %head.1 = (f32[64,9504]{1,0:T(8,128)S(1)}, f32[1,128]{1,0:T(1,128)S(1)}) custom-call(bf16[64,896]{1,0:T(8,128)(2,1)} %refs_0_.1, f32[896]{0:T(1024)} %refs_1_.1, bf16[896,38016]{1,0:T(8,128)(2,1)} %refs_2_.1), custom_call_target="tpu_custom_call" | custom-call | tf_op jit(solution)/shard_map/head/pallas_call | solution.py:359
  76.2 0.0 copy-start
  76.2 1.7 %broadcast_subtract_fusion = f32[64,9504]{1,0:T(8,128)} fusion(f32[64,9504]{1,0:T(8,128)S(1)} %get-tuple-element.4, f32[64]{0:T(128)S(1)} %slice_bitcast_fusion), kind=kLoop, calls=%fused_computation | loop fusion | flops 608256 | bytes 4866304 | tf_op jit(solution)/shard_map/sub | solution.py:391
  77.9 0.0 copy-done
  (1 shorter events, 0.0 us)
Async XLA Ops:
  76.2 1.7 %copy-start = (f32[64]{0:T(128)}, f32[64]{0:T(128)S(1)}, u32[]{:S(2)}) copy-start(f32[64]{0:T(128)S(1)} %slice_bitcast_fusion) | copy-start | bytes 772

commit v11 on v10

--- a/solution.py
+++ b/solution.py
@@ -10,6 +10,7 @@
 LANES = 128
 TILES = 3
 CHUNK = TILES * LANES
+AHEAD = 3
 SLOTS = 3
 RELAY_AT = (4, 10)
 
@@ -244,8 +245,12 @@
     def _():
         relay_copy(0).start()
 
-    across_step(2, 1)
-    across_copy(1).start()
+    @pl.loop(2, AHEAD + 2)
+    def _(t):
+        far_step(t + 2, t + 1)
+        across_step(t, t - 1)
+        across_copy(t - 1).start()
+
     mate_step(0)
     mate_step(1)
     own_step(0)
@@ -253,14 +258,16 @@
 
     @pl.loop(1, end)
     def _(i):
-        @pl.when(i < end - 2)
-        def _():
-            far_step(i + 3, i + 2)
-
-        @pl.when(i < end - 1)
-        def _():
-            across_step(i + 2, i + 1)
-            across_copy(i + 1).start()
+        t = i + AHEAD + 1
+
+        @pl.when(t + 2 <= end)
+        def _():
+            far_step(t + 2, t + 1)
+
+        @pl.when(t <= end)
+        def _():
+            across_step(t, t - 1)
+            across_copy(t - 1).start()
 
         mate_step(i + 1)
         own_step(i)

time: 78 us -> 71.6 us (0.918)
  Pallas kernels: 75.6 us -> 69.1 us
    pallas_call x1, Pallas kernels: 75.6 us -> 69.1 us  [local_head(): pl.pallas_call(body, out_shape=(jax.ShapeDtypeStruct((rows, width), jnp.f...]
where the time goes in v11:
time: 71.6 us; the launch traced here: 71.4 us
  Pallas kernels  69.1 us (97%)
  other arithmetic  1.67 us (2%)
    pallas_call x1, Pallas kernels, local_head(): pl.pallas_call(body, out_shape=(jax.ShapeDtypeStruct((rows, width), jnp.f...  69.1 us
    sub x1, other arithmetic, local_head(): return (z - log_norm[:, None], log_norm)  1.67 us

profile of v11, /device:TPU:0, one launch (start us, length us, event | category | flops | bytes accessed | tf_op | source)
XLA Modules:
  0.0 71.4 jit_solution(8769625163715502342)
XLA Ops:
  0.6 69.1 %head.1 = (f32[64,9504]{1,0:T(8,128)S(1)}, f32[1,128]{1,0:T(1,128)S(1)}) custom-call(bf16[64,896]{1,0:T(8,128)(2,1)} %refs_0_.1, f32[896]{0:T(1024)} %refs_1_.1, bf16[896,38016]{1,0:T(8,128)(2,1)} %refs_2_.1), custom_call_target="tpu_custom_call" | custom-call | tf_op jit(solution)/shard_map/head/pallas_call | solution.py:366
  69.7 0.0 copy-start
  69.7 1.7 %broadcast_subtract_fusion = f32[64,9504]{1,0:T(8,128)} fusion(f32[64,9504]{1,0:T(8,128)S(1)} %get-tuple-element.4, f32[64]{0:T(128)S(1)} %slice_bitcast_fusion), kind=kLoop, calls=%fused_computation | loop fusion | flops 608256 | bytes 4866304 | tf_op jit(solution)/shard_map/sub | solution.py:398
  71.4 0.0 copy-done
  (1 shorter events, 0.0 us)
Async XLA Ops:
  69.7 1.7 %copy-start = (f32[64]{0:T(128)}, f32[64]{0:T(128)S(1)}, u32[]{:S(2)}) copy-start(f32[64]{0:T(128)S(1)} %slice_bitcast_fusion) | copy-start | bytes 772

commit v12 on v11

--- a/solution.py
+++ b/solution.py
@@ -11,6 +11,7 @@
 TILES = 3
 CHUNK = TILES * LANES
 AHEAD = 3
+LOCAL = 5
 SLOTS = 3
 RELAY_AT = (4, 10)
 
@@ -251,9 +252,11 @@
         across_step(t, t - 1)
         across_copy(t - 1).start()
 
-    mate_step(0)
-    mate_step(1)
-    own_step(0)
+    @pl.loop(0, LOCAL)
+    def _(i):
+        mate_step(i)
+        own_step(i)
+
     arrive(0, True, False)
 
     @pl.loop(1, end)
@@ -269,8 +272,11 @@
             across_step(t, t - 1)
             across_copy(t - 1).start()
 
-        mate_step(i + 1)
-        own_step(i)
+        @pl.when(i + LOCAL <= end + 1)
+        def _():
+            mate_step(i + LOCAL - 1)
+            own_step(i + LOCAL - 1)
+
         arrive(i, False, False)
 
         @pl.when((i == RELAY_AT[0]) & (col == 0))
@@ -284,7 +290,6 @@
             relay_copy(2).start()
 
     pl.semaphore_wait(hops.at[2], beside)
-    own_step(end)
     arrive(end, False, True)
 
     last = carry[...]

time: 71.6 us -> 71.3 us (level)
  no operation moved by 1% of the time
where the time goes in v12:
time: 71.3 us; the launch traced here: 71.2 us
  Pallas kernels  68.8 us (96%)
  other arithmetic  1.67 us (2%)
    pallas_call x1, Pallas kernels, local_head(): pl.pallas_call(body, out_shape=(jax.ShapeDtypeStruct((rows, width), jnp.f...  68.8 us
    sub x1, other arithmetic, local_head(): return (z - log_norm[:, None], log_norm)  1.67 us

profile of v12, /device:TPU:0, one launch (start us, length us, event | category | flops | bytes accessed | tf_op | source)
XLA Modules:
  0.0 71.2 jit_solution(2697758487087813969)
XLA Ops:
  0.6 68.8 %head.1 = (f32[64,9504]{1,0:T(8,128)S(1)}, f32[1,128]{1,0:T(1,128)S(1)}) custom-call(bf16[64,896]{1,0:T(8,128)(2,1)} %refs_0_.1, f32[896]{0:T(1024)} %refs_1_.1, bf16[896,38016]{1,0:T(8,128)(2,1)} %refs_2_.1), custom_call_target="tpu_custom_call" | custom-call | tf_op jit(solution)/shard_map/head/pallas_call | solution.py:371
  69.5 0.0 copy-start
  69.5 1.7 %broadcast_subtract_fusion = f32[64,9504]{1,0:T(8,128)} fusion(f32[64,9504]{1,0:T(8,128)S(1)} %get-tuple-element.4, f32[64]{0:T(128)S(1)} %slice_bitcast_fusion), kind=kLoop, calls=%fused_computation | loop fusion | flops 608256 | bytes 4866304 | tf_op jit(solution)/shard_map/sub | solution.py:403
  71.2 0.0 copy-done
  (1 shorter events, 0.0 us)
Async XLA Ops:
  69.5 1.7 %copy-start = (f32[64]{0:T(128)}, f32[64]{0:T(128)S(1)}, u32[]{:S(2)}) copy-start(f32[64]{0:T(128)S(1)} %slice_bitcast_fusion) | copy-start | bytes 772

commit v13 on v12

--- a/solution.py
+++ b/solution.py
@@ -10,17 +10,17 @@
 LANES = 128
 TILES = 3
 CHUNK = TILES * LANES
-AHEAD = 3
-LOCAL = 5
-SLOTS = 3
-RELAY_AT = (4, 10)
+SLOTS = 4
+GROUPS = ((0,), (1, 2), (3, 7), (8, 17), (18, 23), (24,))
+RELAY = 12
+RELAY_AT = 14
 
 
 def head_kernel(
     count, width, hidden_size,
     h_hbm, g_hbm, w_ref, z_ref, lse_ref,
     h_ref, g_ref, wq, wr, wp, wl, x_ref, qbuf, rbuf, pbuf, lbuf, rin, lin, yin, nst, fst, m_ref, s_ref, carry, edge_out, edge_in, relay_in, relay_mid,
-    h_sem, g_sem, hops, wq_sem, wr_sem, wp_sem, wl_sem, nsend, nrecv, qsend, psend, ysend, rrecv, lrecv, yrecv, fsend, frecv, esend, erecv, tail_send, tail_recv, relay_send, relay_recv,
+    h_sem, g_sem, hops, wq_sem, wr_sem, wp_sem, wl_sem, nsend, nrecv, qsend, psend, ysend, rrecv, lrecv, yrecv, fsend, frecv, esend, erecv, relay_send, relay_recv,
 ):
     rows, feats = h_ref.shape
     stride = (width // LANES) * LANES
@@ -39,11 +39,16 @@
         "far": (far, wq, wq_sem), "across": (across, wr, wr_sem), "mate": (mate, wp, wp_sem), "own": (row, wl, wl_sem)
     }
 
+    def chunk_at(t):
+        if isinstance(t, int) and t < 2:
+            return t * RELAY
+        return t - 1 + t // (RELAY + 1)
+
     def fetch(name, t):
         part, buf, sem = streams[name]
         chunk = t
         if name in ("far", "across"):
-            chunk = (0, end)[t] if isinstance(t, int) and t < 2 else t - 1
+            chunk = chunk_at(t)
         start = pl.multiple_of(stride * part + CHUNK * chunk, LANES)
         slot = lax.rem(t, SLOTS)
         return pltpu.make_async_copy(w_ref.at[:, pl.ds(start, CHUNK)], buf.at[slot], sem.at[slot])
@@ -87,7 +92,9 @@
 
     for k in (2, 3, 1):
         norm_copy(k).start()
-    for name, t in (("far", 2), ("across", 1), ("across", 2), *[(n, t) for t in range(SLOTS) for n in ("mate", "own")]):
+    for name, t in (
+        *[(n, t) for t in range(1, SLOTS) for n in ("far", "across") if n == "across" or t > 1], *[(n, t) for t in range(SLOTS) for n in ("mate", "own")]
+    ):
         fetch(name, t).start()
     for k in range(1, 4):
         peer = lax.rem(row + k, 4)
@@ -118,38 +125,49 @@
             device_id={"row": mate}, device_id_type=MESH,
         )
 
-    def across_copy(i):
+    most = pl.ds(0, (TILES - 1) * LANES)
+    final = len(GROUPS) - 1
+
+    def across_copy(k, where):
         return pltpu.make_async_remote_copy(
-            src_ref=rbuf.at[i], dst_ref=yin.at[i], send_sem=ysend.at[i], recv_sem=yrecv.at[i],
+            src_ref=rbuf.at[where], dst_ref=yin.at[where], send_sem=ysend.at[k], recv_sem=yrecv.at[k],
             device_id={"row": across}, device_id_type=MESH,
         )
 
-    most = pl.ds(0, (TILES - 1) * LANES)
-
-    def tail_copy(lanes):
-        return pltpu.make_async_remote_copy(
-            src_ref=rbuf.at[end, :, lanes], dst_ref=yin.at[end, :, lanes], send_sem=tail_send, recv_sem=tail_recv,
-            device_id={"row": across}, device_id_type=MESH,
-        )
-
-    def each_tail(act):
-        @pl.when((col < 3) & (core == 0))
-        def _():
-            act(tail_copy(most))
-
-        @pl.when((col < 3) & (core == 1))
-        def _():
-            act(tail_copy(pl.ds(0, CHUNK)))
-
-        @pl.when((col == 3) & (core == 1))
-        def _():
-            act(tail_copy(pl.ds((TILES - 1) * LANES, LANES)))
+    def pieces(k):
+        lo, hi = GROUPS[k][0], GROUPS[k][-1]
+        if lo <= RELAY <= hi:
+            return [(k, pl.ds(lo, RELAY - lo)), (len(GROUPS), pl.ds(RELAY + 1, hi - RELAY))]
+        return [(k, pl.ds(lo, hi - lo + 1))]
+
+    def each_group(k, act):
+        if k < final:
+            for sem, where in pieces(k):
+                act(across_copy(sem, where))
+            return
+
+        @pl.when(core == 0)
+        def _():
+            act(across_copy(k, (end, slice(None), most)))
+
+        @pl.when(core == 1)
+        def _():
+            act(across_copy(k, end))
+
+    def each_single(act):
+        @pl.when(col < 3)
+        def _():
+            act(across_copy(len(GROUPS) + 1, RELAY))
+
+        @pl.when(col == 3)
+        def _():
+            act(across_copy(len(GROUPS) + 1, (RELAY, slice(None), pl.ds((TILES - 1) * LANES, LANES))))
 
     def relay_copy(k):
         src, dst, device = (
-            (rbuf.at[end, :, most], relay_in, {"col": 0}),
+            (rbuf.at[RELAY, :, most], relay_in, {"col": 0}),
             (relay_in, relay_mid, {"row": across}),
-            (relay_mid, yin.at[end, :, most], {"col": 3}),
+            (relay_mid, yin.at[RELAY, :, most], {"col": 3}),
         )[k]
         return pltpu.make_async_remote_copy(
             src_ref=src, dst_ref=dst, send_sem=relay_send.at[k], recv_sem=relay_recv.at[k],
@@ -186,14 +204,22 @@
 
     def arrive(i, first, last):
         mate_copy(pbuf, lin, psend, lrecv, i).wait_recv()
-        if last:
-            each_tail(lambda copy: copy.wait_recv())
-
-            @pl.when(col == 3)
+        if first or last:
+            each_group(0 if first else final, lambda copy: copy.wait_recv())
+        else:
+            for k in range(1, final):
+                for sem, where in pieces(k):
+                    @pl.when(i == where.start)
+                    def _():
+                        across_copy(sem, where).wait_recv()
+
+            @pl.when(i == RELAY)
             def _():
-                relay_copy(2).wait_recv()
-        else:
-            across_copy(i).wait_recv()
+                each_single(lambda copy: copy.wait_recv())
+
+                @pl.when(col == 3)
+                def _():
+                    relay_copy(2).wait_recv()
         full = lbuf[i] + lin[i] + yin[i]
         parts = [full[:, k * LANES:(k + 1) * LANES] for k in range(TILES)]
         if first:
@@ -229,67 +255,61 @@
         m_ref[...] = top
         s_ref[...] = mass
 
+    far_step(0, 0)
     pl.semaphore_wait(hops.at[0], beside)
     tell_columns(hops.at[1])
-    far_step(0, 0)
-    far_step(1, end)
+    far_step(1, RELAY)
     across_step(0, 0)
-    across_copy(0).start()
+    each_group(0, lambda copy: copy.start())
     far_step(2, 1)
     far_step(3, 2)
-    across_step(1, end)
+    across_step(1, RELAY)
     pl.semaphore_wait(hops.at[1], beside)
     tell_columns(hops.at[2])
-    each_tail(lambda copy: copy.start())
+    each_single(lambda copy: copy.start())
 
     @pl.when(col == 3)
     def _():
         relay_copy(0).start()
 
-    @pl.loop(2, AHEAD + 2)
+    @pl.loop(2, count)
     def _(t):
-        far_step(t + 2, t + 1)
-        across_step(t, t - 1)
-        across_copy(t - 1).start()
-
-    @pl.loop(0, LOCAL)
+        @pl.when(t < end - 1)
+        def _():
+            far_step(t + 2, chunk_at(t + 2))
+
+        i = chunk_at(t)
+        across_step(t, i)
+        for k in range(1, final):
+            for sem, where in pieces(k):
+                @pl.when(i == where.start + where.size - 1)
+                def _():
+                    across_copy(sem, where).start()
+
+        @pl.when((t == RELAY_AT) & (col == 0))
+        def _():
+            relay_copy(0).wait_recv()
+            relay_copy(1).start()
+
+    each_group(final, lambda copy: copy.start())
+
+    @pl.loop(0, count)
     def _(i):
         mate_step(i)
         own_step(i)
 
+    @pl.when(col == 0)
+    def _():
+        relay_copy(1).wait_recv()
+        relay_copy(2).start()
+
+    pl.semaphore_wait(hops.at[2], beside)
     arrive(0, True, False)
 
     @pl.loop(1, end)
     def _(i):
-        t = i + AHEAD + 1
-
-        @pl.when(t + 2 <= end)
-        def _():
-            far_step(t + 2, t + 1)
-
-        @pl.when(t <= end)
-        def _():
-            across_step(t, t - 1)
-            across_copy(t - 1).start()
-
-        @pl.when(i + LOCAL <= end + 1)
-        def _():
-            mate_step(i + LOCAL - 1)
-            own_step(i + LOCAL - 1)
-
         arrive(i, False, False)
 
-        @pl.when((i == RELAY_AT[0]) & (col == 0))
-        def _():
-            relay_copy(0).wait_recv()
-            relay_copy(1).start()
-
-        @pl.when((i == RELAY_AT[1]) & (col == 0))
-        def _():
-            relay_copy(1).wait_recv()
-            relay_copy(2).start()
-
-    pl.semaphore_wait(hops.at[2], beside)
     arrive(end, False, True)
 
     last = carry[...]
@@ -334,11 +354,9 @@
             src_ref=src, dst_ref=dst, send_sem=send, recv_sem=recv.at[0],
             device_id={"row": mate}, device_id_type=MESH,
         ).wait_send()
-    @pl.loop(0, end)
-    def _(i):
-        across_copy(i).wait_send()
-
-    each_tail(lambda copy: copy.wait_send())
+    for k in range(len(GROUPS)):
+        each_group(k, lambda copy: copy.wait_send())
+    each_single(lambda copy: copy.wait_send())
 
     @pl.when(col == 3)
     def _():
@@ -392,7 +410,7 @@
                 *[pltpu.VMEM((rows, (TILES - 1) * LANES), jnp.float32) for _ in range(2)],
                 dma, dma, pltpu.SemaphoreType.REGULAR((3,)),
                 *[dma((SLOTS,)) for _ in range(4)], dma((4,)), dma((4,)),
-                dma, dma, dma((count,)), dma((count,)), dma((count,)), dma((count,)), dma((16,)), dma((16,)), dma, dma, dma, dma, dma((3,)), dma((3,)),
+                dma, dma, dma((len(GROUPS) + 2,)), dma((count,)), dma((count,)), dma((len(GROUPS) + 2,)), dma((16,)), dma((16,)), dma, dma, dma((3,)), dma((3,)),
             ],
             compiler_params=pltpu.CompilerParams(
                 collective_id=0, has_side_effects=True, vmem_limit_bytes=48 * 1024 * 1024

time: 71.3 us -> 70.8 us (level)
  no operation moved by 1% of the time
where the time goes in v13:
time: 70.8 us; the launch traced here: 70.6 us
  Pallas kernels  68.3 us (96%)
  other arithmetic  1.67 us (2%)
    pallas_call x1, Pallas kernels, local_head(): pl.pallas_call(body, out_shape=(jax.ShapeDtypeStruct((rows, width), jnp.f...  68.3 us
    sub x1, other arithmetic, local_head(): return (z - log_norm[:, None], log_norm)  1.67 us

profile of v13, /device:TPU:0, one launch (start us, length us, event | category | flops | bytes accessed | tf_op | source)
XLA Modules:
  0.0 70.6 jit_solution(12092608083975842377)
XLA Ops:
  0.6 68.3 %head.1 = (f32[64,9504]{1,0:T(8,128)S(1)}, f32[1,128]{1,0:T(1,128)S(1)}) custom-call(bf16[64,896]{1,0:T(8,128)(2,1)} %refs_0_.1, f32[896]{0:T(1024)} %refs_1_.1, bf16[896,38016]{1,0:T(8,128)(2,1)} %refs_2_.1), custom_call_target="tpu_custom_call" | custom-call | tf_op jit(solution)/shard_map/head/pallas_call | solution.py:389
  68.9 0.0 copy-start
  68.9 1.7 %broadcast_subtract_fusion = f32[64,9504]{1,0:T(8,128)} fusion(f32[64,9504]{1,0:T(8,128)S(1)} %get-tuple-element.4, f32[64]{0:T(128)S(1)} %slice_bitcast_fusion), kind=kLoop, calls=%fused_computation | loop fusion | flops 608256 | bytes 4866304 | tf_op jit(solution)/shard_map/sub | solution.py:421
  70.6 0.0 copy-done
  (1 shorter events, 0.0 us)
Async XLA Ops:
  68.9 1.7 %copy-start = (f32[64]{0:T(128)}, f32[64]{0:T(128)S(1)}, u32[]{:S(2)}) copy-start(f32[64]{0:T(128)S(1)} %slice_bitcast_fusion) | copy-start | bytes 772

commit v14 on v13

--- a/solution.py
+++ b/solution.py
@@ -55,16 +55,21 @@
 
     barrier = pltpu.get_barrier_semaphore()
 
+    def tell_column(sem, step):
+        @pl.when((col + step >= 0) & (col + step < 4))
+        def _():
+            pl.semaphore_signal(sem, inc=1, device_id_type=MESH, device_id={"col": col + step})
+
     def tell_columns(sem):
-        for step, there in ((-1, col > 0), (1, col < 3)):
-            @pl.when(there)
-            def _():
-                pl.semaphore_signal(sem, inc=1, device_id_type=MESH, device_id={"col": col + step})
+        tell_column(sem, -1)
+        tell_column(sem, 1)
 
     for k in (2, 3, 1):
         pl.semaphore_signal(barrier, inc=1, device_id_type=MESH, device_id={"row": lax.rem(row + k, 4)})
-    tell_columns(barrier)
-    beside = (col + 2) // 3 + (5 - col) // 3
+    tell_column(barrier, 1)
+    below = (col + 2) // 3
+    above = (5 - col) // 3
+    beside = below + above
 
     h_copy = pltpu.make_async_copy(h_hbm, h_ref, h_sem)
     g_copy = pltpu.make_async_copy(g_hbm, g_ref, g_sem)
@@ -81,8 +86,8 @@
         sq = sq + part * part
     sq = jnp.transpose(jnp.concatenate([sq, sq], axis=0))
     nst[row] = jnp.sum(sq, axis=0, keepdims=True)
-    pl.semaphore_wait(barrier, 3 + beside)
-    tell_columns(hops.at[0])
+    pl.semaphore_wait(barrier, 3 + below)
+    tell_column(hops.at[0], -1)
 
     def norm_copy(k):
         return pltpu.make_async_remote_copy(
@@ -256,16 +261,22 @@
         s_ref[...] = mass
 
     far_step(0, 0)
-    pl.semaphore_wait(hops.at[0], beside)
+
+    @pl.when(col < 3)
+    def _():
+        pl.semaphore_wait(hops.at[0], 1)
+
     tell_columns(hops.at[1])
     far_step(1, RELAY)
     across_step(0, 0)
     each_group(0, lambda copy: copy.start())
     far_step(2, 1)
+    pl.semaphore_wait(hops.at[1], beside)
+    tell_columns(hops.at[2])
     far_step(3, 2)
     across_step(1, RELAY)
-    pl.semaphore_wait(hops.at[1], beside)
-    tell_columns(hops.at[2])
+    pl.semaphore_wait(hops.at[2], beside)
+    tell_columns(hops.at[3])
     each_single(lambda copy: copy.start())
 
     @pl.when(col == 3)
@@ -303,7 +314,7 @@
         relay_copy(1).wait_recv()
         relay_copy(2).start()
 
-    pl.semaphore_wait(hops.at[2], beside)
+    pl.semaphore_wait(hops.at[3], beside)
     arrive(0, True, False)
 
     @pl.loop(1, end)
@@ -408,7 +419,7 @@
                 pltpu.VMEM((16, 1, LANES), jnp.float32),
                 *[pltpu.VMEM((rows, LANES), jnp.float32) for _ in range(5)],
                 *[pltpu.VMEM((rows, (TILES - 1) * LANES), jnp.float32) for _ in range(2)],
-                dma, dma, pltpu.SemaphoreType.REGULAR((3,)),
+                dma, dma, pltpu.SemaphoreType.REGULAR((4,)),
                 *[dma((SLOTS,)) for _ in range(4)], dma((4,)), dma((4,)),
                 dma, dma, dma((len(GROUPS) + 2,)), dma((count,)), dma((count,)), dma((len(GROUPS) + 2,)), dma((16,)), dma((16,)), dma, dma, dma((3,)), dma((3,)),
             ],

time: 70.8 us -> 70.2 us (level)
  no operation moved by 1% of the time
where the time goes in v14:
time: 70.2 us; the launch traced here: 70.1 us
  Pallas kernels  67.7 us (96%)
  other arithmetic  1.67 us (2%)
    pallas_call x1, Pallas kernels, local_head(): pl.pallas_call(body, out_shape=(jax.ShapeDtypeStruct((rows, width), jnp.f...  67.7 us
    sub x1, other arithmetic, local_head(): return (z - log_norm[:, None], log_norm)  1.67 us

profile of v14, /device:TPU:0, one launch (start us, length us, event | category | flops | bytes accessed | tf_op | source)
XLA Modules:
  0.0 70.1 jit_solution(6202470259456327391)
XLA Ops:
  0.6 67.7 %head.1 = (f32[64,9504]{1,0:T(8,128)S(1)}, f32[1,128]{1,0:T(1,128)S(1)}) custom-call(bf16[64,896]{1,0:T(8,128)(2,1)} %refs_0_.1, f32[896]{0:T(1024)} %refs_1_.1, bf16[896,38016]{1,0:T(8,128)(2,1)} %refs_2_.1), custom_call_target="tpu_custom_call" | custom-call | tf_op jit(solution)/shard_map/head/pallas_call | solution.py:400
  68.4 0.0 copy-start
  68.4 1.7 %broadcast_subtract_fusion = f32[64,9504]{1,0:T(8,128)} fusion(f32[64,9504]{1,0:T(8,128)S(1)} %get-tuple-element.4, f32[64]{0:T(128)S(1)} %slice_bitcast_fusion), kind=kLoop, calls=%fused_computation | loop fusion | flops 608256 | bytes 4866304 | tf_op jit(solution)/shard_map/sub | solution.py:432
  70.1 0.0 copy-done
  (1 shorter events, 0.0 us)
Async XLA Ops:
  68.4 1.7 %copy-start = (f32[64]{0:T(128)}, f32[64]{0:T(128)S(1)}, u32[]{:S(2)}) copy-start(f32[64]{0:T(128)S(1)} %slice_bitcast_fusion) | copy-start | bytes 772

commit v15 on v14

--- a/solution.py
+++ b/solution.py
@@ -19,8 +19,8 @@
 def head_kernel(
     count, width, hidden_size,
     h_hbm, g_hbm, w_ref, z_ref, lse_ref,
-    h_ref, g_ref, wq, wr, wp, wl, x_ref, qbuf, rbuf, pbuf, lbuf, rin, lin, yin, nst, fst, m_ref, s_ref, carry, edge_out, edge_in, relay_in, relay_mid,
-    h_sem, g_sem, hops, wq_sem, wr_sem, wp_sem, wl_sem, nsend, nrecv, qsend, psend, ysend, rrecv, lrecv, yrecv, fsend, frecv, esend, erecv, relay_send, relay_recv,
+    h_ref, g_ref, wq, wr, wp, wl, x_ref, qbuf, rbuf, pbuf, lbuf, rin, lin, yin, nst, fst, m_ref, s_ref, carry, edge_out, edge_in, relay_in, relay_mid, rx, qx,
+    h_sem, g_sem, hops, wq_sem, wr_sem, wp_sem, wl_sem, nsend, nrecv, qsend, psend, ysend, rrecv, lrecv, yrecv, fsend, frecv, esend, erecv, relay_send, relay_recv, rx_send, rx_recv, qx_send,
 ):
     rows, feats = h_ref.shape
     stride = (width // LANES) * LANES
@@ -145,19 +145,35 @@
             return [(k, pl.ds(lo, RELAY - lo)), (len(GROUPS), pl.ds(RELAY + 1, hi - RELAY))]
         return [(k, pl.ds(lo, hi - lo + 1))]
 
+    rx_copy = pltpu.make_async_remote_copy(
+        src_ref=rbuf.at[end, :, most], dst_ref=rx, send_sem=rx_send, recv_sem=rx_recv,
+        device_id={"row": mate}, device_id_type=MESH,
+    )
+    qx_copy = pltpu.make_async_remote_copy(
+        src_ref=qx, dst_ref=yin.at[end, :, most], send_sem=qx_send, recv_sem=yrecv.at[final],
+        device_id={"row": far}, device_id_type=MESH,
+    )
+
+    def last_step():
+        rbuf[end] = product("across", end)
+
+        @pl.when(core == 0)
+        def _():
+            rx_copy.start()
+
+        mate_copy(qbuf, rin, qsend, rrecv, end).wait_recv()
+
+        @pl.when(core == 1)
+        def _():
+            rx_copy.wait_recv()
+            qx[...] = qbuf[end, :, most] + rx[...]
+            qx_copy.start()
+            rbuf[end] = rbuf[end] + rin[end]
+            across_copy(final, end).start()
+
     def each_group(k, act):
-        if k < final:
-            for sem, where in pieces(k):
-                act(across_copy(sem, where))
-            return
-
-        @pl.when(core == 0)
-        def _():
-            act(across_copy(k, (end, slice(None), most)))
-
-        @pl.when(core == 1)
-        def _():
-            act(across_copy(k, end))
+        for sem, where in pieces(k):
+            act(across_copy(sem, where))
 
     def each_single(act):
         @pl.when(col < 3)
@@ -209,8 +225,16 @@
 
     def arrive(i, first, last):
         mate_copy(pbuf, lin, psend, lrecv, i).wait_recv()
-        if first or last:
-            each_group(0 if first else final, lambda copy: copy.wait_recv())
+        if first:
+            each_group(0, lambda copy: copy.wait_recv())
+        elif last:
+            @pl.when(core == 0)
+            def _():
+                qx_copy.wait_recv()
+
+            @pl.when(core == 1)
+            def _():
+                across_copy(final, end).wait_recv()
         else:
             for k in range(1, final):
                 for sem, where in pieces(k):
@@ -283,7 +307,7 @@
     def _():
         relay_copy(0).start()
 
-    @pl.loop(2, count)
+    @pl.loop(2, end)
     def _(t):
         @pl.when(t < end - 1)
         def _():
@@ -302,7 +326,7 @@
             relay_copy(0).wait_recv()
             relay_copy(1).start()
 
-    each_group(final, lambda copy: copy.start())
+    last_step()
 
     @pl.loop(0, count)
     def _(i):
@@ -335,23 +359,23 @@
     me = col * 4 + row
     fst[me] = jnp.where(lane[:1] < rows, peak, mass)
 
-    peers = [
-        (c, lax.rem(row + dr, 4))
-        for c in (3 - col, lax.rem(col + 2, 4), lax.rem(5 - col, 4), col) for dr in (2, 3, 1, 0)
-    ][:-1]
-
-    def stat_copy(k, slot):
-        c, r = peers[k]
+    def stat_copy(c, dr, slot):
         return pltpu.make_async_remote_copy(
-            src_ref=fst.at[slot], dst_ref=fst.at[slot], send_sem=fsend.at[k], recv_sem=frecv.at[slot],
-            device_id={"col": c, "row": r}, device_id_type=MESH,
+            src_ref=fst.at[slot], dst_ref=fst.at[slot], send_sem=fsend.at[c * 4 + dr], recv_sem=frecv.at[slot],
+            device_id={"col": c, "row": lax.rem(row + dr, 4)}, device_id_type=MESH,
         )
 
-    for k in range(15):
-        stat_copy(k, me).start()
-    for k in reversed(range(15)):
-        c, r = peers[k]
-        stat_copy(k, c * 4 + r).wait_recv()
+    def each_peer(act):
+        for c in range(4):
+            for dr in (2, 3, 1):
+                act(c, dr)
+
+            @pl.when(col != c)
+            def _():
+                act(c, 0)
+
+    each_peer(lambda c, dr: stat_copy(c, dr, me).start())
+    each_peer(lambda c, dr: stat_copy(c, dr, c * 4 + lax.rem(row + dr, 4)).wait_recv())
     stats = fst[...]
     swapped = pltpu.roll(stats, LANES // 2, 2)
     peak = jnp.max(stats, axis=0)
@@ -365,10 +389,19 @@
             src_ref=src, dst_ref=dst, send_sem=send, recv_sem=recv.at[0],
             device_id={"row": mate}, device_id_type=MESH,
         ).wait_send()
-    for k in range(len(GROUPS)):
+    for k in range(final):
         each_group(k, lambda copy: copy.wait_send())
     each_single(lambda copy: copy.wait_send())
 
+    @pl.when(core == 0)
+    def _():
+        rx_copy.wait_send()
+
+    @pl.when(core == 1)
+    def _():
+        qx_copy.wait_send()
+        across_copy(final, end).wait_send()
+
     @pl.when(col == 3)
     def _():
         relay_copy(0).wait_send()
@@ -382,8 +415,7 @@
     def _():
         edge_copy.wait_send()
 
-    for k in range(15):
-        stat_copy(k, me).wait_send()
+    each_peer(lambda c, dr: stat_copy(c, dr, me).wait_send())
 
 
 def solution(mesh):
@@ -418,10 +450,10 @@
                 pltpu.VMEM((4, 1, LANES), jnp.float32),
                 pltpu.VMEM((16, 1, LANES), jnp.float32),
                 *[pltpu.VMEM((rows, LANES), jnp.float32) for _ in range(5)],
-                *[pltpu.VMEM((rows, (TILES - 1) * LANES), jnp.float32) for _ in range(2)],
+                *[pltpu.VMEM((rows, (TILES - 1) * LANES), jnp.float32) for _ in range(4)],
                 dma, dma, pltpu.SemaphoreType.REGULAR((4,)),
                 *[dma((SLOTS,)) for _ in range(4)], dma((4,)), dma((4,)),
-                dma, dma, dma((len(GROUPS) + 2,)), dma((count,)), dma((count,)), dma((len(GROUPS) + 2,)), dma((16,)), dma((16,)), dma, dma, dma((3,)), dma((3,)),
+                dma, dma, dma((len(GROUPS) + 2,)), dma((count,)), dma((count,)), dma((len(GROUPS) + 2,)), dma((16,)), dma((16,)), dma, dma, dma((3,)), dma((3,)), dma, dma, dma,
             ],
             compiler_params=pltpu.CompilerParams(
                 collective_id=0, has_side_effects=True, vmem_limit_bytes=48 * 1024 * 1024

time: 70.2 us -> 69.7 us (level)
  no operation moved by 1% of the time
where the time goes in v15:
time: 69.7 us; the launch traced here: 69.5 us
  Pallas kernels  67.2 us (96%)
  other arithmetic  1.67 us (2%)
    pallas_call x1, Pallas kernels, local_head(): pl.pallas_call(body, out_shape=(jax.ShapeDtypeStruct((rows, width), jnp.f...  67.2 us
    sub x1, other arithmetic, local_head(): return (z - log_norm[:, None], log_norm)  1.67 us

profile of v15, /device:TPU:0, one launch (start us, length us, event | category | flops | bytes accessed | tf_op | source)
XLA Modules:
  0.0 69.5 jit_solution(4914071968928241345)
XLA Ops:
  0.6 67.2 %head.1 = (f32[64,9504]{1,0:T(8,128)S(1)}, f32[1,128]{1,0:T(1,128)S(1)}) custom-call(bf16[64,896]{1,0:T(8,128)(2,1)} %refs_0_.1, f32[896]{0:T(1024)} %refs_1_.1, bf16[896,38016]{1,0:T(8,128)(2,1)} %refs_2_.1), custom_call_target="tpu_custom_call" | custom-call | tf_op jit(solution)/shard_map/head/pallas_call | solution.py:432
  67.8 0.0 copy-start
  67.9 1.7 %broadcast_subtract_fusion = f32[64,9504]{1,0:T(8,128)} fusion(f32[64,9504]{1,0:T(8,128)S(1)} %get-tuple-element.4, f32[64]{0:T(128)S(1)} %slice_bitcast_fusion), kind=kLoop, calls=%fused_computation | loop fusion | flops 608256 | bytes 4866304 | tf_op jit(solution)/shard_map/sub | solution.py:464
  69.5 0.0 copy-done
  (1 shorter events, 0.0 us)
Async XLA Ops:
  67.8 1.7 %copy-start = (f32[64]{0:T(128)}, f32[64]{0:T(128)S(1)}, u32[]{:S(2)}) copy-start(f32[64]{0:T(128)S(1)} %slice_bitcast_fusion) | copy-start | bytes 772

commit v16 on v15

--- a/solution.py
+++ b/solution.py
@@ -11,7 +11,7 @@
 TILES = 3
 CHUNK = TILES * LANES
 SLOTS = 4
-GROUPS = ((0,), (1, 2), (3, 7), (8, 17), (18, 23), (24,))
+GROUPS = ((0,), (1, 4), (5, 18), (19, 23), (24,))
 RELAY = 12
 RELAY_AT = 14
 
@@ -19,8 +19,8 @@
 def head_kernel(
     count, width, hidden_size,
     h_hbm, g_hbm, w_ref, z_ref, lse_ref,
-    h_ref, g_ref, wq, wr, wp, wl, x_ref, qbuf, rbuf, pbuf, lbuf, rin, lin, yin, nst, fst, m_ref, s_ref, carry, edge_out, edge_in, relay_in, relay_mid, rx, qx,
-    h_sem, g_sem, hops, wq_sem, wr_sem, wp_sem, wl_sem, nsend, nrecv, qsend, psend, ysend, rrecv, lrecv, yrecv, fsend, frecv, esend, erecv, relay_send, relay_recv, rx_send, rx_recv, qx_send,
+    h_ref, g_ref, wq, wr, wp, wl, x_ref, qbuf, rbuf, pbuf, lbuf, rin, lin, yin, nst, fst, m_ref, s_ref, carry, edge_out, edge_in, relay_in, relay_mid, rx, qx, first_in,
+    h_sem, g_sem, hops, wq_sem, wr_sem, wp_sem, wl_sem, nsend, nrecv, qsend, psend, ysend, rrecv, lrecv, yrecv, fsend, frecv, esend, erecv, relay_send, relay_recv, rx_send, rx_recv, qx_send, first_send, first_recv,
 ):
     rows, feats = h_ref.shape
     stride = (width // LANES) * LANES
@@ -154,6 +154,20 @@
         device_id={"row": far}, device_id_type=MESH,
     )
 
+    lead = pl.ds(0, LANES)
+    rest_of = pl.ds(LANES, (TILES - 1) * LANES)
+
+    def first_copy(k):
+        src, dst, device = (
+            (qbuf.at[0, :, lead], first_in, far),
+            (rbuf.at[0, :, lead], yin.at[0, :, lead], across),
+            (rbuf.at[0, :, rest_of], yin.at[0, :, rest_of], across),
+        )[k]
+        return pltpu.make_async_remote_copy(
+            src_ref=src, dst_ref=dst, send_sem=first_send.at[k], recv_sem=first_recv.at[k],
+            device_id={"row": device}, device_id_type=MESH,
+        )
+
     def last_step():
         rbuf[end] = product("across", end)
 
@@ -226,7 +240,8 @@
     def arrive(i, first, last):
         mate_copy(pbuf, lin, psend, lrecv, i).wait_recv()
         if first:
-            each_group(0, lambda copy: copy.wait_recv())
+            for k in range(3):
+                first_copy(k).wait_recv()
         elif last:
             @pl.when(core == 0)
             def _():
@@ -252,6 +267,7 @@
         full = lbuf[i] + lin[i] + yin[i]
         parts = [full[:, k * LANES:(k + 1) * LANES] for k in range(TILES)]
         if first:
+            parts[0] = parts[0] + first_in[...]
             edge_out[...] = parts[0]
 
             @pl.when(core == 1)
@@ -285,6 +301,10 @@
         s_ref[...] = mass
 
     far_step(0, 0)
+    first_copy(0).start()
+    rbuf[0] = product("across", 0)
+    first_copy(1).start()
+    refill("across", 0)
 
     @pl.when(col < 3)
     def _():
@@ -292,8 +312,9 @@
 
     tell_columns(hops.at[1])
     far_step(1, RELAY)
-    across_step(0, 0)
-    each_group(0, lambda copy: copy.start())
+    mate_copy(qbuf, rin, qsend, rrecv, 0).wait_recv()
+    rbuf[0, :, LANES:] = rbuf[0, :, LANES:] + rin[0, :, LANES:]
+    first_copy(2).start()
     far_step(2, 1)
     pl.semaphore_wait(hops.at[1], beside)
     tell_columns(hops.at[2])
@@ -389,7 +410,9 @@
             src_ref=src, dst_ref=dst, send_sem=send, recv_sem=recv.at[0],
             device_id={"row": mate}, device_id_type=MESH,
         ).wait_send()
-    for k in range(final):
+    for k in range(3):
+        first_copy(k).wait_send()
+    for k in range(1, final):
         each_group(k, lambda copy: copy.wait_send())
     each_single(lambda copy: copy.wait_send())
 
@@ -451,9 +474,11 @@
                 pltpu.VMEM((16, 1, LANES), jnp.float32),
                 *[pltpu.VMEM((rows, LANES), jnp.float32) for _ in range(5)],
                 *[pltpu.VMEM((rows, (TILES - 1) * LANES), jnp.float32) for _ in range(4)],
+                pltpu.VMEM((rows, LANES), jnp.float32),
                 dma, dma, pltpu.SemaphoreType.REGULAR((4,)),
                 *[dma((SLOTS,)) for _ in range(4)], dma((4,)), dma((4,)),
                 dma, dma, dma((len(GROUPS) + 2,)), dma((count,)), dma((count,)), dma((len(GROUPS) + 2,)), dma((16,)), dma((16,)), dma, dma, dma((3,)), dma((3,)), dma, dma, dma,
+                dma((3,)), dma((3,)),
             ],
             compiler_params=pltpu.CompilerParams(
                 collective_id=0, has_side_effects=True, vmem_limit_bytes=48 * 1024 * 1024

time: 69.7 us -> 69.9 us (level)
  no operation moved by 1% of the time
where the time goes in v16:
time: 69.9 us; the launch traced here: 69.7 us
  Pallas kernels  67.4 us (96%)
  other arithmetic  1.67 us (2%)
    pallas_call x1, Pallas kernels, local_head(): pl.pallas_call(body, out_shape=(jax.ShapeDtypeStruct((rows, width), jnp.f...  67.4 us
    sub x1, other arithmetic, local_head(): return (z - log_norm[:, None], log_norm)  1.67 us

profile of v16, /device:TPU:0, one launch (start us, length us, event | category | flops | bytes accessed | tf_op | source)
XLA Modules:
  0.0 69.7 jit_solution(11539451010318355303)
XLA Ops:
  0.6 67.4 %head.1 = (f32[64,9504]{1,0:T(8,128)S(1)}, f32[1,128]{1,0:T(1,128)S(1)}) custom-call(bf16[64,896]{1,0:T(8,128)(2,1)} %refs_0_.1, f32[896]{0:T(1024)} %refs_1_.1, bf16[896,38016]{1,0:T(8,128)(2,1)} %refs_2_.1), custom_call_target="tpu_custom_call" | custom-call | tf_op jit(solution)/shard_map/head/pallas_call | solution.py:455
  68.1 0.0 copy-start
  68.1 1.7 %broadcast_subtract_fusion = f32[64,9504]{1,0:T(8,128)} fusion(f32[64,9504]{1,0:T(8,128)S(1)} %get-tuple-element.4, f32[64]{0:T(128)S(1)} %slice_bitcast_fusion), kind=kLoop, calls=%fused_computation | loop fusion | flops 608256 | bytes 4866304 | tf_op jit(solution)/shard_map/sub | solution.py:489
  69.7 0.0 copy-done
  (1 shorter events, 0.0 us)
Async XLA Ops:
  68.1 1.7 %copy-start = (f32[64]{0:T(128)}, f32[64]{0:T(128)S(1)}, u32[]{:S(2)}) copy-start(f32[64]{0:T(128)S(1)} %slice_bitcast_fusion) | copy-start | bytes 772

commit v17 on v16

--- a/solution.py
+++ b/solution.py
@@ -11,7 +11,7 @@
 TILES = 3
 CHUNK = TILES * LANES
 SLOTS = 4
-GROUPS = ((0,), (1, 4), (5, 18), (19, 23), (24,))
+GROUPS = ((0,), (1, 2), (3, 7), (8, 17), (18, 23), (24,))
 RELAY = 12
 RELAY_AT = 14
 

time: 69.9 us -> 69.4 us (level)
  no operation moved by 1% of the time
where the time goes in v17:
time: 69.4 us; the launch traced here: 69.3 us
  Pallas kernels  66.9 us (96%)
  other arithmetic  1.67 us (2%)
    pallas_call x1, Pallas kernels, local_head(): pl.pallas_call(body, out_shape=(jax.ShapeDtypeStruct((rows, width), jnp.f...  66.9 us
    sub x1, other arithmetic, local_head(): return (z - log_norm[:, None], log_norm)  1.67 us

profile of v17, /device:TPU:0, one launch (start us, length us, event | category | flops | bytes accessed | tf_op | source)
XLA Modules:
  0.0 69.3 jit_solution(15849447827060428644)
XLA Ops:
  0.6 66.9 %head.1 = (f32[64,9504]{1,0:T(8,128)S(1)}, f32[1,128]{1,0:T(1,128)S(1)}) custom-call(bf16[64,896]{1,0:T(8,128)(2,1)} %refs_0_.1, f32[896]{0:T(1024)} %refs_1_.1, bf16[896,38016]{1,0:T(8,128)(2,1)} %refs_2_.1), custom_call_target="tpu_custom_call" | custom-call | tf_op jit(solution)/shard_map/head/pallas_call | solution.py:455
  67.6 0.0 copy-start
  67.6 1.7 %broadcast_subtract_fusion = f32[64,9504]{1,0:T(8,128)} fusion(f32[64,9504]{1,0:T(8,128)S(1)} %get-tuple-element.4, f32[64]{0:T(128)S(1)} %slice_bitcast_fusion), kind=kLoop, calls=%fused_computation | loop fusion | flops 608256 | bytes 4866304 | tf_op jit(solution)/shard_map/sub | solution.py:489
  69.3 0.0 copy-done
  (1 shorter events, 0.0 us)
Async XLA Ops:
  67.6 1.7 %copy-start = (f32[64]{0:T(128)}, f32[64]{0:T(128)S(1)}, u32[]{:S(2)}) copy-start(f32[64]{0:T(128)S(1)} %slice_bitcast_fusion) | copy-start | bytes 772

commit v18 on v17

--- a/solution.py
+++ b/solution.py
@@ -200,7 +200,7 @@
 
     def relay_copy(k):
         src, dst, device = (
-            (rbuf.at[RELAY, :, most], relay_in, {"col": 0}),
+            (rbuf.at[RELAY, :, most], relay_in, {"col": core}),
             (relay_in, relay_mid, {"row": across}),
             (relay_mid, yin.at[RELAY, :, most], {"col": 3}),
         )[k]
@@ -342,7 +342,7 @@
                 def _():
                     across_copy(sem, where).start()
 
-        @pl.when((t == RELAY_AT) & (col == 0))
+        @pl.when((t == RELAY_AT) & (col == core))
         def _():
             relay_copy(0).wait_recv()
             relay_copy(1).start()
@@ -354,7 +354,7 @@
         mate_step(i)
         own_step(i)
 
-    @pl.when(col == 0)
+    @pl.when(col == core)
     def _():
         relay_copy(1).wait_recv()
         relay_copy(2).start()
@@ -429,7 +429,7 @@
     def _():
         relay_copy(0).wait_send()
 
-    @pl.when(col == 0)
+    @pl.when(col == core)
     def _():
         relay_copy(1).wait_send()
         relay_copy(2).wait_send()

time: 69.4 us -> 69.3 us (level)
  no operation moved by 1% of the time
where the time goes in v18:
time: 69.3 us; the launch traced here: 69.1 us
  Pallas kernels  66.8 us (96%)
  other arithmetic  1.67 us (2%)
    pallas_call x1, Pallas kernels, local_head(): pl.pallas_call(body, out_shape=(jax.ShapeDtypeStruct((rows, width), jnp.f...  66.8 us
    sub x1, other arithmetic, local_head(): return (z - log_norm[:, None], log_norm)  1.67 us

profile of v18, /device:TPU:0, one launch (start us, length us, event | category | flops | bytes accessed | tf_op | source)
XLA Modules:
  0.0 69.1 jit_solution(17142015159390250937)
XLA Ops:
  0.6 66.8 %head.1 = (f32[64,9504]{1,0:T(8,128)S(1)}, f32[1,128]{1,0:T(1,128)S(1)}) custom-call(bf16[64,896]{1,0:T(8,128)(2,1)} %refs_0_.1, f32[896]{0:T(1024)} %refs_1_.1, bf16[896,38016]{1,0:T(8,128)(2,1)} %refs_2_.1), custom_call_target="tpu_custom_call" | custom-call | tf_op jit(solution)/shard_map/head/pallas_call | solution.py:455
  67.5 0.0 copy-start
  67.5 1.7 %broadcast_subtract_fusion = f32[64,9504]{1,0:T(8,128)} fusion(f32[64,9504]{1,0:T(8,128)S(1)} %get-tuple-element.4, f32[64]{0:T(128)S(1)} %slice_bitcast_fusion), kind=kLoop, calls=%fused_computation | loop fusion | flops 608256 | bytes 4866304 | tf_op jit(solution)/shard_map/sub | solution.py:489
  69.1 0.0 copy-done
  (1 shorter events, 0.0 us)
Async XLA Ops:
  67.5 1.7 %copy-start = (f32[64]{0:T(128)}, f32[64]{0:T(128)S(1)}, u32[]{:S(2)}) copy-start(f32[64]{0:T(128)S(1)} %slice_bitcast_fusion) | copy-start | bytes 772

commit v19 on v18

--- a/solution.py
+++ b/solution.py
@@ -189,20 +189,23 @@
         for sem, where in pieces(k):
             act(across_copy(sem, where))
 
+    late = col >= 3 - core
+    early = col <= core
+
     def each_single(act):
-        @pl.when(col < 3)
+        @pl.when(jnp.logical_not(late))
         def _():
             act(across_copy(len(GROUPS) + 1, RELAY))
 
-        @pl.when(col == 3)
+        @pl.when(late)
         def _():
             act(across_copy(len(GROUPS) + 1, (RELAY, slice(None), pl.ds((TILES - 1) * LANES, LANES))))
 
     def relay_copy(k):
         src, dst, device = (
-            (rbuf.at[RELAY, :, most], relay_in, {"col": core}),
+            (rbuf.at[RELAY, :, most], relay_in, {"col": core * (col - 2)}),
             (relay_in, relay_mid, {"row": across}),
-            (relay_mid, yin.at[RELAY, :, most], {"col": 3}),
+            (relay_mid, yin.at[RELAY, :, most], {"col": 3 + core * (col - 1)}),
         )[k]
         return pltpu.make_async_remote_copy(
             src_ref=src, dst_ref=dst, send_sem=relay_send.at[k], recv_sem=relay_recv.at[k],
@@ -261,7 +264,7 @@
             def _():
                 each_single(lambda copy: copy.wait_recv())
 
-                @pl.when(col == 3)
+                @pl.when(late)
                 def _():
                     relay_copy(2).wait_recv()
         full = lbuf[i] + lin[i] + yin[i]
@@ -324,7 +327,7 @@
     tell_columns(hops.at[3])
     each_single(lambda copy: copy.start())
 
-    @pl.when(col == 3)
+    @pl.when(late)
     def _():
         relay_copy(0).start()
 
@@ -342,7 +345,7 @@
                 def _():
                     across_copy(sem, where).start()
 
-        @pl.when((t == RELAY_AT) & (col == core))
+        @pl.when((t == RELAY_AT) & early)
         def _():
             relay_copy(0).wait_recv()
             relay_copy(1).start()
@@ -354,7 +357,7 @@
         mate_step(i)
         own_step(i)
 
-    @pl.when(col == core)
+    @pl.when(early)
     def _():
         relay_copy(1).wait_recv()
         relay_copy(2).start()
@@ -380,23 +383,21 @@
     me = col * 4 + row
     fst[me] = jnp.where(lane[:1] < rows, peak, mass)
 
-    def stat_copy(c, dr, slot):
-        return pltpu.make_async_remote_copy(
-            src_ref=fst.at[slot], dst_ref=fst.at[slot], send_sem=fsend.at[c * 4 + dr], recv_sem=frecv.at[slot],
-            device_id={"col": c, "row": lax.rem(row + dr, 4)}, device_id_type=MESH,
+    def stat_copy(c, r, slot):
+        return pltpu.make_async_remote_copy(
+            src_ref=fst.at[slot], dst_ref=fst.at[slot], send_sem=fsend.at[c * 4 + r], recv_sem=frecv.at[slot],
+            device_id={"col": c, "row": r}, device_id_type=MESH,
         )
 
     def each_peer(act):
         for c in range(4):
-            for dr in (2, 3, 1):
-                act(c, dr)
-
-            @pl.when(col != c)
-            def _():
-                act(c, 0)
-
-    each_peer(lambda c, dr: stat_copy(c, dr, me).start())
-    each_peer(lambda c, dr: stat_copy(c, dr, c * 4 + lax.rem(row + dr, 4)).wait_recv())
+            for r in range(4):
+                @pl.when(me != c * 4 + r)
+                def _():
+                    act(c, r)
+
+    each_peer(lambda c, r: stat_copy(c, r, me).start())
+    each_peer(lambda c, r: stat_copy(c, r, c * 4 + r).wait_recv())
     stats = fst[...]
     swapped = pltpu.roll(stats, LANES // 2, 2)
     peak = jnp.max(stats, axis=0)
@@ -425,11 +426,11 @@
         qx_copy.wait_send()
         across_copy(final, end).wait_send()
 
-    @pl.when(col == 3)
+    @pl.when(late)
     def _():
         relay_copy(0).wait_send()
 
-    @pl.when(col == core)
+    @pl.when(early)
     def _():
         relay_copy(1).wait_send()
         relay_copy(2).wait_send()
@@ -438,7 +439,7 @@
     def _():
         edge_copy.wait_send()
 
-    each_peer(lambda c, dr: stat_copy(c, dr, me).wait_send())
+    each_peer(lambda c, r: stat_copy(c, r, me).wait_send())
 
 
 def solution(mesh):

time: 69.3 us -> 69.4 us (level)
  no operation moved by 1% of the time
where the time goes in v19:
time: 69.4 us; the launch traced here: 69.3 us
  Pallas kernels  66.9 us (96%)
  other arithmetic  1.67 us (2%)
    pallas_call x1, Pallas kernels, local_head(): pl.pallas_call(body, out_shape=(jax.ShapeDtypeStruct((rows, width), jnp.f...  66.9 us
    sub x1, other arithmetic, local_head(): return (z - log_norm[:, None], log_norm)  1.67 us

profile of v19, /device:TPU:0, one launch (start us, length us, event | category | flops | bytes accessed | tf_op | source)
XLA Modules:
  0.0 69.3 jit_solution(7880205143750463298)
XLA Ops:
  0.6 66.9 %head.1 = (f32[64,9504]{1,0:T(8,128)S(1)}, f32[1,128]{1,0:T(1,128)S(1)}) custom-call(bf16[64,896]{1,0:T(8,128)(2,1)} %refs_0_.1, f32[896]{0:T(1024)} %refs_1_.1, bf16[896,38016]{1,0:T(8,128)(2,1)} %refs_2_.1), custom_call_target="tpu_custom_call" | custom-call | tf_op jit(solution)/shard_map/head/pallas_call | solution.py:456
  67.6 0.0 copy-start
  67.6 1.7 %broadcast_subtract_fusion = f32[64,9504]{1,0:T(8,128)} fusion(f32[64,9504]{1,0:T(8,128)S(1)} %get-tuple-element.4, f32[64]{0:T(128)S(1)} %slice_bitcast_fusion), kind=kLoop, calls=%fused_computation | loop fusion | flops 608256 | bytes 4866304 | tf_op jit(solution)/shard_map/sub | solution.py:490
  69.3 0.0 copy-done
  (1 shorter events, 0.0 us)
Async XLA Ops:
  67.6 1.7 %copy-start = (f32[64]{0:T(128)}, f32[64]{0:T(128)S(1)}, u32[]{:S(2)}) copy-start(f32[64]{0:T(128)S(1)} %slice_bitcast_fusion) | copy-start | bytes 772

commit v20 on v19

--- a/solution.py
+++ b/solution.py
@@ -11,7 +11,7 @@
 TILES = 3
 CHUNK = TILES * LANES
 SLOTS = 4
-GROUPS = ((0,), (1, 2), (3, 7), (8, 17), (18, 23), (24,))
+GROUPS = ((0,), (1, 2), (3, 7), (8, 17), (18, 22), (23,), (24,))
 RELAY = 12
 RELAY_AT = 14
 
@@ -323,12 +323,11 @@
     tell_columns(hops.at[2])
     far_step(3, 2)
     across_step(1, RELAY)
-    pl.semaphore_wait(hops.at[2], beside)
-    tell_columns(hops.at[3])
     each_single(lambda copy: copy.start())
 
     @pl.when(late)
     def _():
+        pl.semaphore_wait(hops.at[2], beside)
         relay_copy(0).start()
 
     @pl.loop(2, end)
@@ -351,6 +350,12 @@
             relay_copy(1).start()
 
     last_step()
+
+    @pl.when(jnp.logical_not(late))
+    def _():
+        pl.semaphore_wait(hops.at[2], beside)
+
+    tell_columns(hops.at[3])
 
     @pl.loop(0, count)
     def _(i):

time: 69.4 us -> 68.6 us (0.988)
  Pallas kernels: 66.9 us -> 66.1 us
    pallas_call x1, Pallas kernels: 66.9 us -> 66.1 us  [local_head(): pl.pallas_call(body, out_shape=(jax.ShapeDtypeStruct((rows, width), jnp.f...]
where the time goes in v20:
time: 68.6 us; the launch traced here: 68.4 us
  Pallas kernels  66.1 us (96%)
  other arithmetic  1.67 us (2%)
    pallas_call x1, Pallas kernels, local_head(): pl.pallas_call(body, out_shape=(jax.ShapeDtypeStruct((rows, width), jnp.f...  66.1 us
    sub x1, other arithmetic, local_head(): return (z - log_norm[:, None], log_norm)  1.67 us

profile of v20, /device:TPU:0, one launch (start us, length us, event | category | flops | bytes accessed | tf_op | source)
XLA Modules:
  0.0 68.4 jit_solution(1003271448992840880)
XLA Ops:
  0.6 66.1 %head.1 = (f32[64,9504]{1,0:T(8,128)S(1)}, f32[1,128]{1,0:T(1,128)S(1)}) custom-call(bf16[64,896]{1,0:T(8,128)(2,1)} %refs_0_.1, f32[896]{0:T(1024)} %refs_1_.1, bf16[896,38016]{1,0:T(8,128)(2,1)} %refs_2_.1), custom_call_target="tpu_custom_call" | custom-call | tf_op jit(solution)/shard_map/head/pallas_call | solution.py:461
  66.7 0.0 copy-start
  66.7 1.7 %broadcast_subtract_fusion = f32[64,9504]{1,0:T(8,128)} fusion(f32[64,9504]{1,0:T(8,128)S(1)} %get-tuple-element.4, f32[64]{0:T(128)S(1)} %slice_bitcast_fusion), kind=kLoop, calls=%fused_computation | loop fusion | flops 608256 | bytes 4866304 | tf_op jit(solution)/shard_map/sub | solution.py:495
  68.4 0.0 copy-done
  (1 shorter events, 0.0 us)
Async XLA Ops:
  66.7 1.7 %copy-start = (f32[64]{0:T(128)}, f32[64]{0:T(128)S(1)}, u32[]{:S(2)}) copy-start(f32[64]{0:T(128)S(1)} %slice_bitcast_fusion) | copy-start | bytes 772

commit v21 on v20

--- a/solution.py
+++ b/solution.py
@@ -22,6 +22,10 @@
     h_ref, g_ref, wq, wr, wp, wl, x_ref, qbuf, rbuf, pbuf, lbuf, rin, lin, yin, nst, fst, m_ref, s_ref, carry, edge_out, edge_in, relay_in, relay_mid, rx, qx, first_in,
     h_sem, g_sem, hops, wq_sem, wr_sem, wp_sem, wl_sem, nsend, nrecv, qsend, psend, ysend, rrecv, lrecv, yrecv, fsend, frecv, esend, erecv, relay_send, relay_recv, rx_send, rx_recv, qx_send, first_send, first_recv,
 ):
+    h_copy = pltpu.make_async_copy(h_hbm, h_ref, h_sem)
+    g_copy = pltpu.make_async_copy(g_hbm, g_ref, g_sem)
+    h_copy.start()
+    g_copy.start()
     rows, feats = h_ref.shape
     stride = (width // LANES) * LANES
     rest = width - stride
@@ -71,10 +75,6 @@
     above = (5 - col) // 3
     beside = below + above
 
-    h_copy = pltpu.make_async_copy(h_hbm, h_ref, h_sem)
-    g_copy = pltpu.make_async_copy(g_hbm, g_ref, g_sem)
-    h_copy.start()
-    g_copy.start()
     h_copy.wait()
     for name, t in (("far", 0), ("far", 1), ("across", 0)):
         fetch(name, t).start()
@@ -402,7 +402,9 @@
                     act(c, r)
 
     each_peer(lambda c, r: stat_copy(c, r, me).start())
-    each_peer(lambda c, r: stat_copy(c, r, c * 4 + r).wait_recv())
+    for k in range(1, 16):
+        peer = lax.rem(me + k, 16)
+        stat_copy(col, row, peer).wait_recv()
     stats = fst[...]
     swapped = pltpu.roll(stats, LANES // 2, 2)
     peak = jnp.max(stats, axis=0)

time: 68.6 us -> 68.5 us (level)
  no operation moved by 1% of the time
where the time goes in v21:
time: 68.5 us; the launch traced here: 68.3 us
  Pallas kernels  66 us (96%)
  other arithmetic  1.67 us (2%)
    pallas_call x1, Pallas kernels, local_head(): pl.pallas_call(body, out_shape=(jax.ShapeDtypeStruct((rows, width), jnp.f...  66 us
    sub x1, other arithmetic, local_head(): return (z - log_norm[:, None], log_norm)  1.67 us

profile of v21, /device:TPU:0, one launch (start us, length us, event | category | flops | bytes accessed | tf_op | source)
XLA Modules:
  0.0 68.3 jit_solution(2326504592926231931)
XLA Ops:
  0.6 66.0 %head.1 = (f32[64,9504]{1,0:T(8,128)S(1)}, f32[1,128]{1,0:T(1,128)S(1)}) custom-call(bf16[64,896]{1,0:T(8,128)(2,1)} %refs_0_.1, f32[896]{0:T(1024)} %refs_1_.1, bf16[896,38016]{1,0:T(8,128)(2,1)} %refs_2_.1), custom_call_target="tpu_custom_call" | custom-call | tf_op jit(solution)/shard_map/head/pallas_call | solution.py:463
  66.7 0.0 copy-start
  66.7 1.7 %broadcast_subtract_fusion = f32[64,9504]{1,0:T(8,128)} fusion(f32[64,9504]{1,0:T(8,128)S(1)} %get-tuple-element.4, f32[64]{0:T(128)S(1)} %slice_bitcast_fusion), kind=kLoop, calls=%fused_computation | loop fusion | flops 608256 | bytes 4866304 | tf_op jit(solution)/shard_map/sub | solution.py:497
  68.3 0.0 copy-done
  (1 shorter events, 0.0 us)
Async XLA Ops:
  66.7 1.7 %copy-start = (f32[64]{0:T(128)}, f32[64]{0:T(128)S(1)}, u32[]{:S(2)}) copy-start(f32[64]{0:T(128)S(1)} %slice_bitcast_fusion) | copy-start | bytes 772

commit v22 on v21

--- a/solution.py
+++ b/solution.py
@@ -11,8 +11,8 @@
 TILES = 3
 CHUNK = TILES * LANES
 SLOTS = 4
-GROUPS = ((0,), (1, 2), (3, 7), (8, 17), (18, 22), (23,), (24,))
-RELAY = 12
+GROUPS = ((0,), (1, 2), (3, 6), (8, 17), (18, 22), (23,), (24,))
+RELAY = 7
 RELAY_AT = 14
 
 
@@ -46,7 +46,7 @@
     def chunk_at(t):
         if isinstance(t, int) and t < 2:
             return t * RELAY
-        return t - 1 + t // (RELAY + 1)
+        return t - 1 + (t + end - RELAY) // count
 
     def fetch(name, t):
         part, buf, sem = streams[name]
@@ -87,7 +87,6 @@
     sq = jnp.transpose(jnp.concatenate([sq, sq], axis=0))
     nst[row] = jnp.sum(sq, axis=0, keepdims=True)
     pl.semaphore_wait(barrier, 3 + below)
-    tell_column(hops.at[0], -1)
 
     def norm_copy(k):
         return pltpu.make_async_remote_copy(
@@ -97,6 +96,7 @@
 
     for k in (2, 3, 1):
         norm_copy(k).start()
+    tell_column(hops.at[0], -1)
     for name, t in (
         *[(n, t) for t in range(1, SLOTS) for n in ("far", "across") if n == "across" or t > 1], *[(n, t) for t in range(SLOTS) for n in ("mate", "own")]
     ):

time: 68.5 us -> 68.5 us (level)
  no operation moved by 1% of the time
where the time goes in v22:
time: 68.5 us; the launch traced here: 68.3 us
  Pallas kernels  66 us (96%)
  other arithmetic  1.67 us (2%)
    pallas_call x1, Pallas kernels, local_head(): pl.pallas_call(body, out_shape=(jax.ShapeDtypeStruct((rows, width), jnp.f...  66 us
    sub x1, other arithmetic, local_head(): return (z - log_norm[:, None], log_norm)  1.67 us

profile of v22, /device:TPU:0, one launch (start us, length us, event | category | flops | bytes accessed | tf_op | source)
XLA Modules:
  0.0 68.3 jit_solution(4624958814418626454)
XLA Ops:
  0.6 66.0 %head.1 = (f32[64,9504]{1,0:T(8,128)S(1)}, f32[1,128]{1,0:T(1,128)S(1)}) custom-call(bf16[64,896]{1,0:T(8,128)(2,1)} %refs_0_.1, f32[896]{0:T(1024)} %refs_1_.1, bf16[896,38016]{1,0:T(8,128)(2,1)} %refs_2_.1), custom_call_target="tpu_custom_call" | custom-call | tf_op jit(solution)/shard_map/head/pallas_call | solution.py:463
  66.6 0.0 copy-start
  66.7 1.7 %broadcast_subtract_fusion = f32[64,9504]{1,0:T(8,128)} fusion(f32[64,9504]{1,0:T(8,128)S(1)} %get-tuple-element.4, f32[64]{0:T(128)S(1)} %slice_bitcast_fusion), kind=kLoop, calls=%fused_computation | loop fusion | flops 608256 | bytes 4866304 | tf_op jit(solution)/shard_map/sub | solution.py:497
  68.3 0.0 copy-done
  (1 shorter events, 0.0 us)
Async XLA Ops:
  66.6 1.7 %copy-start = (f32[64]{0:T(128)}, f32[64]{0:T(128)S(1)}, u32[]{:S(2)}) copy-start(f32[64]{0:T(128)S(1)} %slice_bitcast_fusion) | copy-start | bytes 772

commit v23 on v22

--- a/solution.py
+++ b/solution.py
@@ -97,10 +97,10 @@
     for k in (2, 3, 1):
         norm_copy(k).start()
     tell_column(hops.at[0], -1)
-    for name, t in (
-        *[(n, t) for t in range(1, SLOTS) for n in ("far", "across") if n == "across" or t > 1], *[(n, t) for t in range(SLOTS) for n in ("mate", "own")]
-    ):
-        fetch(name, t).start()
+    for t in range(1, SLOTS):
+        if t > 1:
+            fetch("far", t).start()
+        fetch("across", t).start()
     for k in range(1, 4):
         peer = lax.rem(row + k, 4)
         pltpu.make_async_remote_copy(
@@ -318,6 +318,9 @@
     mate_copy(qbuf, rin, qsend, rrecv, 0).wait_recv()
     rbuf[0, :, LANES:] = rbuf[0, :, LANES:] + rin[0, :, LANES:]
     first_copy(2).start()
+    for t in range(SLOTS):
+        fetch("mate", t).start()
+        fetch("own", t).start()
     far_step(2, 1)
     pl.semaphore_wait(hops.at[1], beside)
     tell_columns(hops.at[2])

time: 68.5 us -> 68.5 us (level)
  no operation moved by 1% of the time
where the time goes in v23:
time: 68.5 us; the launch traced here: 68.3 us
  Pallas kernels  66 us (96%)
  other arithmetic  1.67 us (2%)
    pallas_call x1, Pallas kernels, local_head(): pl.pallas_call(body, out_shape=(jax.ShapeDtypeStruct((rows, width), jnp.f...  66 us
    sub x1, other arithmetic, local_head(): return (z - log_norm[:, None], log_norm)  1.67 us

profile of v23, /device:TPU:0, one launch (start us, length us, event | category | flops | bytes accessed | tf_op | source)
XLA Modules:
  0.0 68.3 jit_solution(12101743652900521189)
XLA Ops:
  0.6 66.0 %head.1 = (f32[64,9504]{1,0:T(8,128)S(1)}, f32[1,128]{1,0:T(1,128)S(1)}) custom-call(bf16[64,896]{1,0:T(8,128)(2,1)} %refs_0_.1, f32[896]{0:T(1024)} %refs_1_.1, bf16[896,38016]{1,0:T(8,128)(2,1)} %refs_2_.1), custom_call_target="tpu_custom_call" | custom-call | tf_op jit(solution)/shard_map/head/pallas_call | solution.py:466
  66.6 0.0 copy-start
  66.7 1.7 %broadcast_subtract_fusion = f32[64,9504]{1,0:T(8,128)} fusion(f32[64,9504]{1,0:T(8,128)S(1)} %get-tuple-element.4, f32[64]{0:T(128)S(1)} %slice_bitcast_fusion), kind=kLoop, calls=%fused_computation | loop fusion | flops 608256 | bytes 4866304 | tf_op jit(solution)/shard_map/sub | solution.py:500
  68.3 0.0 copy-done
  (1 shorter events, 0.0 us)
Async XLA Ops:
  66.6 1.7 %copy-start = (f32[64]{0:T(128)}, f32[64]{0:T(128)S(1)}, u32[]{:S(2)}) copy-start(f32[64]{0:T(128)S(1)} %slice_bitcast_fusion) | copy-start | bytes 772
